TPU v7x, 256 devices: a whole 4x4x8 slice. The times are simulated.
256 devices in a mesh: tm: 4 (over y), blk: 64 (over x, z, core).
Axes of the slice: x: 4, y: 4, z: 8, core: 2. Of those that a mesh axis runs over, the one named last changes fastest.
Arguments:
- chi_bar: bfloat16 [4, 64, 24, 128, 128], P('tm', 'blk'), may hold values from -0.023925781 to 0.023925781
- cos_table: int32 [8, 4], replicated, may hold values from -1024 to 1024
- partner: int32 [64, 24], P('blk'), may hold values from 0 to 63, all different within a row
- tensor: bfloat16 [8192, 2, 2048], P('blk'), may hold values from -6 to 6
- dens_tensor: bfloat16 [8192, 2, 2048], P('blk'), may hold values from -6 to 6
- decay: float32 [8, 2, 2048], P('tm'), may hold values from 0.1 to 1
Outputs:
- tensor_grad: bfloat16 [8, 8192, 2, 2048], P('tm', 'blk')
- density_grad: float32 [8192, 128], P('blk')
Inputs may be any that keep to these rules, and one draw needn't show every extreme that they name: `partner`: each row names 24 different blocks; every block is named by some row.
All inputs are finite; a program needn't handle non-finite values.
Results may differ from a plain program's by a relative error of at most 0.011.
Values may be sent and summed in bfloat16 or wider, within the bound.
No kernel may reach another device: no remote copies, remote signals or barrier semaphores. Data moves between devices by JAX's collectives and lax.ppermute only.
A program may use at most 64 MiB of HBM per device.

v0:
```python
import math

import jax
import jax.numpy as jnp
from jax import lax
from jax.experimental import pallas as pl
from jax.experimental.pallas import tpu as pltpu
from jax.sharding import PartitionSpec as P


CHUNKS = (64, 64)
LAST_BY_GROUP = True
NX, NZ, NC, NY = 4, 8, 2, 4

bf16 = jnp.bfloat16
f32 = jnp.float32
VMEM = pltpu.VMEM
SMEM = pltpu.SMEM


def blk_of(x, z, c):
    return (x * NZ + z) * NC + c


CHIPS = [(x, z) for x in range(NX) for z in range(NZ)]
CORE_SWAP = [(blk_of(x, z, c), blk_of(x, z, 1 - c)) for x, z in CHIPS for c in range(NC)]
Z_GROUPS = [[blk_of(x, z, c) for z in range(NZ)] for x in range(NX) for c in range(NC)]


def x_shift(d):
    return [(blk_of(x, z, c), blk_of((x + d) % NX, z, c)) for x, z in CHIPS for c in range(NC)]


def z_shift(d):
    return [(blk_of(x, z, c), blk_of(x, (z + d) % NZ, c)) for x, z in CHIPS for c in range(NC)]


def y_shift(d):
    return [(i, (i + d) % NY) for i in range(NY)]


def call(body, out_shape, *args, smem=(), flops=0, mib=16):
    many = isinstance(out_shape, (list, tuple))
    size = sum(math.prod(a.shape) * a.dtype.itemsize for a in args)
    out_spec = pl.BlockSpec(memory_space=VMEM)
    return pl.pallas_call(
        body,
        out_shape=out_shape,
        in_specs=[pl.BlockSpec(memory_space=SMEM if i in smem else VMEM) for i in range(len(args))],
        out_specs=[out_spec] * len(out_shape) if many else out_spec,
        cost_estimate=pl.CostEstimate(flops=flops, bytes_accessed=size, transcendentals=0),
        compiler_params=pltpu.CompilerParams(vmem_limit_bytes=mib << 20),
    )(*args)


def prep_body(tens_ref, dens_ref, decay_ref, metric_ref, gram_ref):
    nt = (((1,), (1,)), ((), ()))
    inv_width = 1.0 / math.sqrt(tens_ref.shape[1])
    tens = tens_ref[...]
    for t in range(decay_ref.shape[0]):
        factor = decay_ref[pl.ds(t, 1), :]
        s = (tens.astype(f32) * factor).astype(bf16)
        d = (dens_ref[...].astype(f32) * factor).astype(bf16)
        m = lax.dot_general(tens, d, nt, preferred_element_type=f32)
        metric_ref[t] = (m * inv_width).astype(bf16)
        for i, left in enumerate((s, d)):
            g = lax.dot_general(left, d, nt, preferred_element_type=f32) * inv_width
            hi = g.astype(bf16)
            gram_ref[t, i, :, 0:128] = hi
            gram_ref[t, i, :, 128:256] = (g - hi.astype(f32)).astype(bf16)


def term_body(part_ref, cos_ref, metric_ref, *refs):
    chi_refs, (send_ref, keep_ref) = (refs[0:4], refs[4:8]), refs[8:]
    half, rows = refs[0].shape[0], refs[0].shape[1]
    group = 6
    me_y = lax.axis_index("tm")
    my_core = lax.axis_index("blk") & 1
    spare = keep_ref.shape[0] - 1
    zero = jnp.zeros((rows, 128), bf16)
    weights = [
        [cos_ref[me_y * 2 + t, (me_y + d) & 3].astype(f32) * (1.0 / 1024.0) for d in (0, 3, 1, 2)]
        for t in range(2)
    ]

    def clear(s, _):
        for t in range(2):
            send_ref[s, t] = zero
            keep_ref[s, t] = zero
        return 0

    lax.fori_loop(0, send_ref.shape[0], clear, 0)
    for k0 in range(0, 2 * half, group):
        ks = slice(k0 % half, k0 % half + group)
        chis = [r[ks].astype(f32) for r in chi_refs[k0 // half]]
        for t in range(2):
            mixed = chis[0] * weights[t][0]
            for i in range(1, 4):
                mixed = mixed + chis[i] * weights[t][i]
            mixed = mixed.astype(bf16).reshape(group * rows, 128)
            prod = jnp.dot(mixed, metric_ref[t], preferred_element_type=f32).astype(bf16)
            for j in range(group):
                p = part_ref[0, k0 + j]
                piece = prod[j * rows : (j + 1) * rows]
                own = (p & 1) == my_core
                keep_ref[jnp.where(own, p >> 1, spare), t] = piece
                send_ref[jnp.where(own, spare, p >> 1), t] = piece


def add_rows(a_ref, b_ref, i):
    return (a_ref[i].astype(f32) + b_ref[i].astype(f32)).astype(bf16)


def add_split_body(a_ref, b_ref, *out_refs):
    my_x = lax.axis_index("blk") >> 4
    for d, out_ref in enumerate(out_refs):
        first = ((my_x + d) & 3) * NZ

        def body(i, _):
            out_ref[i] = add_rows(a_ref, b_ref, first + i)
            return 0

        lax.fori_loop(0, NZ, body, 0, unroll=4)


def sum_split_body(a_ref, b_ref, c_ref, d_ref, *out_refs):
    my_z = (lax.axis_index("blk") >> 1) & 7
    for d, out_ref in enumerate(out_refs):
        i = (my_z + d) & 7
        low = a_ref[i].astype(f32) + b_ref[i].astype(f32)
        out_ref[...] = (low + (c_ref[i].astype(f32) + d_ref[i].astype(f32))).astype(bf16)


def sum_body(a_ref, b_ref, c_ref, d_ref, out_ref):
    def body(i, _):
        low = a_ref[i].astype(f32) + b_ref[i].astype(f32)
        out_ref[i] = (low + (c_ref[i].astype(f32) + d_ref[i].astype(f32))).astype(bf16)
        return 0

    lax.fori_loop(0, NZ, body, 0, unroll=4)


def sum_all_body(*refs):
    total = refs[0][...].astype(f32)
    for r in refs[1:-1]:
        total = total + r[...].astype(f32)
    refs[-1][...] = total.astype(bf16)


def sum_lead_body(in_ref, out_ref):
    step = 16
    for t in range(out_ref.shape[0]):
        for r in range(0, out_ref.shape[1], step):
            rows = slice(r, r + step)
            total = in_ref[0, t, rows].astype(f32)
            for i in range(1, in_ref.shape[0]):
                total = total + in_ref[i, t, rows].astype(f32)
            out_ref[t, rows] = total.astype(bf16)


def spread(c, side):
    shape = (2 * c.shape[0], c.shape[0])
    r = lax.broadcasted_iota(jnp.int32, shape, 0)
    a = lax.broadcasted_iota(jnp.int32, shape, 1)
    pick = jnp.where((r >> 1) == a, 1.0, 0.0).astype(bf16)
    c = lax.dot_general(pick, c, (((1,), (side,)), ((), ())), preferred_element_type=f32)
    even = (r & 1) == 0
    return jnp.concatenate([jnp.where(even, c, 0.0), jnp.where(even, 0.0, c)], axis=1).astype(bf16)


def gather_rows(col_refs, t):
    return jnp.concatenate([r[t] for r in col_refs], axis=0)


def final_body(tens0_ref, tens1_ref, dens0_ref, dens1_ref, decay0_ref, decay1_ref, *refs):
    col_refs, grad_ref, mix_ref = refs[:-2], refs[-2], refs[-1]
    times = grad_ref.shape[0]

    @pl.when(pl.program_id(0) == 0)
    def _():
        for t in range(times):
            c = gather_rows(col_refs, t)
            for side in range(2):
                mix_ref[t, side] = spread(c, side)

    def scaled(refs, t):
        return jnp.concatenate(
            [(r[...].astype(f32) * f[pl.ds(t, 1), :]).astype(bf16) for r, f in zip(refs, (decay0_ref, decay1_ref))], axis=0
        )

    for t in range(times):
        g = jnp.dot(mix_ref[t, 0], scaled((tens0_ref, tens1_ref), t), preferred_element_type=f32)
        g = g + jnp.dot(mix_ref[t, 1], scaled((dens0_ref, dens1_ref), t), preferred_element_type=f32)
        grad_ref[t] = g.astype(bf16).reshape(g.shape[0] // 2, 2, g.shape[1])


def final(tens, dens, decay, collected):
    block, width = tens.shape
    times = decay.shape[0]
    half, step = width // 2, 512
    steps = half // step
    views = [pl.BlockSpec((block, step), lambda i, j=j: (0, i + j * steps)) for j in range(2)]
    decays = [pl.BlockSpec((times, step), lambda i, j=j: (0, i + j * steps)) for j in range(2)]
    whole = [pl.BlockSpec(c.shape, lambda i: (0, 0, 0)) for c in collected]
    return pl.pallas_call(
        final_body,
        grid=(steps,),
        out_shape=sds((times, block, 2, half)),
        in_specs=views * 2 + decays + whole,
        out_specs=pl.BlockSpec((times, block, 2, step), lambda i: (0, 0, 0, i)),
        scratch_shapes=[VMEM((times, 2, 2 * block, 2 * block), bf16)],
        cost_estimate=pl.CostEstimate(flops=10**9, bytes_accessed=4 << 20, transcendentals=0),
        compiler_params=pltpu.CompilerParams(vmem_limit_bytes=16 << 20),
        name="final",
    )(tens, tens, dens, dens, decay, decay, *collected)


def density_body(gram_ref, *refs):
    col_refs, out_ref = refs[:-1], refs[-1]
    tn = (((0,), (0,)), ((), ()))
    total = jnp.zeros((128, 256), f32)
    for t in range(2):
        c = gather_rows(col_refs, t)
        total = total + jnp.dot(c, gram_ref[t, 0], preferred_element_type=f32)
        total = total + lax.dot_general(c, gram_ref[t, 1], tn, preferred_element_type=f32)
    out_ref[...] = (total[:, 0:128] + total[:, 128:256]).astype(bf16)


def density_sum_body(a_ref, b_ref, c_ref, d_ref, out_ref):
    out_ref[...] = (a_ref[...].astype(f32) + b_ref[...].astype(f32)) + (c_ref[...].astype(f32) + d_ref[...].astype(f32))


def sds(shape, dtype=bf16):
    return jax.ShapeDtypeStruct(shape, dtype)


def exchange(value, groups):
    return lax.all_to_all(value, "blk", 0, 0, axis_index_groups=groups, tiled=True)


def work(chi_bar, cos_table, partner, tensor, dens_tensor, decay):
    pairs = chi_bar.shape[2]
    half = pairs // 2
    times = decay.shape[0]
    block = tensor.shape[0]
    width = tensor.shape[1] * tensor.shape[2]
    up, down = y_shift(1), y_shift(-1)

    chis = []
    start = 0
    for rows in CHUNKS:
        mine = [chi_bar[0, 0, h : h + half, start : start + rows, :] for h in (0, half)]
        low_a = lax.ppermute(mine[0], "tm", up)
        high_b = lax.ppermute(mine[1], "tm", down)
        low_b = lax.ppermute(mine[1], "tm", up)
        high_a = lax.ppermute(mine[0], "tm", down)
        far_a = lax.ppermute(low_a, "tm", up)
        far_b = lax.ppermute(high_b, "tm", down)
        chis.append((mine[0], low_a, high_a, far_a, mine[1], low_b, high_b, far_b))
        start += rows

    inputs = (tensor.reshape(block, width), dens_tensor.reshape(block, width), decay.reshape(times, width))
    metric, gram = call(
        prep_body, [sds((times, block, block)), sds((times, 2, block, 2 * block))], *inputs, flops=10**9
    )
    collected = []
    for c, rows in enumerate(CHUNKS):
        shape = sds((NX * NZ + 1, times, rows, block))
        piece = sds((NZ, times, rows, block))
        small = sds((times, rows, block))
        send, keep = call(term_body, [shape, shape], partner, cos_table, metric, *chis[c], smem=(0, 1), flops=10**9)
        other = lax.ppermute(send, "blk", CORE_SWAP)
        both = call(add_split_body, [piece] * NX, keep, other, flops=10**7)
        moved = [lax.ppermute(both[d], "blk", x_shift(d)) for d in range(1, NX)]
        if c == 0 or not LAST_BY_GROUP:
            both = call(sum_split_body, [small] * NZ, both[0], *moved, flops=10**7)
            moved = [lax.ppermute(both[d], "blk", z_shift(d)) for d in range(1, NZ)]
            collected.append(call(sum_all_body, small, both[0], *moved, flops=10**7))
        else:
            both = call(sum_body, piece, both[0], *moved, flops=10**7)
            both = exchange(both, Z_GROUPS)
            collected.append(call(sum_lead_body, small, both, flops=10**7))
    dpart = call(density_body, sds((block, block)), gram, *collected, flops=10**8)
    parts = [lax.ppermute(dpart, "tm", y_shift(d)) for d in range(1, NY)]
    grad = final(*inputs, collected)
    density = call(density_sum_body, sds((block, block), f32), dpart, *parts)
    return (grad, density)


def solution(mesh):
    return jax.shard_map(
        work,
        mesh=mesh,
        in_specs=(
            P("tm", "blk", None, None, None),
            P(),
            P("blk", None),
            P("blk", None, None),
            P("blk", None, None),
            P("tm", None, None),
        ),
        out_specs=(P("tm", "blk", None, None), P("blk", None)),
        check_vma=False,
    )
```

profile of v0, /device:TPU:2, one launch (start us, length us, event | category | flops | bytes accessed | tf_op | source)
XLA Modules:
  0.0 114.1 jit_solution(15202222420931587393)
XLA Ops:
  2.0 1.7 %collective-permute-start.17 = (bf16[12,64,128]{2,1,0:T(8,128)(2,1)S(1)}, bf16[12,64,128]{2,1,0:T(8,128)(2,1)}, u32[]{:S(2)}, u32[]{:S(2)}) collective-permute-start(bf16[12,64,128]{2,1,0:T(8,128)(2,1)S(1)} %get-tuple-element.49.refs_0_), channel_id=1, source_target_pairs={{0,64},{64,128},{128,192},{192,0},{1,65},{65,129},{129,193},{193,1... | collective-permute-start | bytes 589832 | tf_op jit(solution)/shard_map/ppermute | solution.py:253
  3.7 1.7 %collective-permute-start.21 = (bf16[12,64,128]{2,1,0:T(8,128)(2,1)S(1)}, bf16[12,64,128]{2,1,0:T(8,128)(2,1)}, u32[]{:S(2)}, u32[]{:S(2)}) collective-permute-start(bf16[12,64,128]{2,1,0:T(8,128)(2,1)S(1)} %get-tuple-element.46.refs_4_), channel_id=1, source_target_pairs={{0,192},{64,0},{128,64},{192,128},{1,193},{65,1},{129,65},{193,129... | collective-permute-start | bytes 589832 | tf_op jit(solution)/shard_map/ppermute | solution.py:254
  5.3 1.8 %collective-permute-start.18 = (bf16[12,64,128]{2,1,0:T(8,128)(2,1)S(1)}, bf16[12,64,128]{2,1,0:T(8,128)(2,1)S(1)}, u32[]{:S(2)}, u32[]{:S(2)}) collective-permute-start(bf16[12,64,128]{2,1,0:T(8,128)(2,1)S(1)} %get-tuple-element.49.refs_0_), channel_id=1, source_target_pairs={{0,192},{64,0},{128,64},{192,128},{1,193},{65,1},{129,65},{193,129... | collective-permute-start | bytes 589832 | tf_op jit(solution)/shard_map/ppermute | solution.py:256
  7.4 2.8 %collective-permute-done.17.refs_1_ = bf16[12,64,128]{2,1,0:T(8,128)(2,1)} collective-permute-done((bf16[12,64,128]{2,1,0:T(8,128)(2,1)S(1)}, bf16[12,64,128]{2,1,0:T(8,128)(2,1)}, u32[]{:S(2)}, u32[]{:S(2)}) %collective-permute-start.17) | collective-permute-done | bytes 196640 | tf_op jit(solution)/shard_map/ppermute | solution.py:253
  11.6 2.9 %collective-permute-start.22 = (bf16[12,64,128]{2,1,0:T(8,128)(2,1)}, bf16[12,64,128]{2,1,0:T(8,128)(2,1)}, u32[]{:S(2)}, u32[]{:S(2)}) collective-permute-start(bf16[12,64,128]{2,1,0:T(8,128)(2,1)} %collective-permute-done.21.refs_6_), channel_id=1, source_target_pairs={{0,192},{64,0},{128,64},{192,128},{1,193},{65,1},{129,65},{193,129... | collective-permute-start | bytes 589832 | tf_op jit(solution)/shard_map/ppermute | solution.py:258
  16.3 3.2 %collective-permute-start.4 = (bf16[12,64,128]{2,1,0:T(8,128)(2,1)S(1)}, bf16[12,64,128]{2,1,0:T(8,128)(2,1)S(1)}, u32[]{:S(2)}, u32[]{:S(2)}) collective-permute-start(bf16[12,64,128]{2,1,0:T(8,128)(2,1)S(1)} %get-tuple-element.47.refs_4_), channel_id=1, source_target_pairs={{0,192},{64,0},{128,64},{192,128},{1,193},{65,1},{129,65},{193,129... | collective-permute-start | bytes 589832 | tf_op jit(solution)/shard_map/ppermute | solution.py:254
  19.5 1.8 %shard_map.77 = (bf16[2,128,128]{2,1,0:T(8,128)(2,1)S(1)}, bf16[2,2,128,256]{3,2,1,0:T(8,128)(2,1)S(1)}) custom-call(bf16[128,4096]{1,0:T(8,128)(2,1)S(1)} %bitcast.14, bf16[128,4096]{1,0:T(8,128)(2,1)S(1)} %bitcast.17, f32[2,4096]{1,0:T(2,128)S(1)} %bitcast.20), custom_call_target="tpu_custom_call" | custom-call | flops 1000000000 | bytes 2129920 | tf_op jit(solution)/shard_map/pallas_call | solution.py:46
  23.1 2.3 %shard_map.82 = (bf16[33,2,64,128]{3,2,1,0:T(8,128)(2,1)S(1)}, bf16[33,2,64,128]{3,2,1,0:T(8,128)(2,1)S(1)}) custom-call(s32[1,24]{1,0:T(1,128)S(1)} %copy-done.8, s32[8,4]{1,0:T(8,128)S(1)} %copy.8.cos_ref, bf16[2,128,128]{2,1,0:T(8,128)(2,1)S(1)} %get-tuple-element.24.metric_ref, bf16[12,64,128]{2,1,0:T(8,128)(2,1)S(1)} %get-tuple-element.49.refs_0_, ...), custom_call_target="tpu_custom_call" | custom-call | flops 1000000000 | bytes 1638624 | tf_op jit(solution)/shard_map/pallas_call | solution.py:46
  26.0 1.7 %collective-permute-start.3 = (bf16[12,64,128]{2,1,0:T(8,128)(2,1)S(1)}, bf16[12,64,128]{2,1,0:T(8,128)(2,1)S(1)}, u32[]{:S(2)}, u32[]{:S(2)}) collective-permute-start(bf16[12,64,128]{2,1,0:T(8,128)(2,1)S(1)} %get-tuple-element.47.refs_4_), channel_id=1, source_target_pairs={{0,64},{64,128},{128,192},{192,0},{1,65},{65,129},{129,193},{193,1... | collective-permute-start | bytes 589832 | tf_op jit(solution)/shard_map/ppermute | solution.py:255
  28.3 3.2 %collective-permute-start.5 = (bf16[12,64,128]{2,1,0:T(8,128)(2,1)S(1)}, bf16[12,64,128]{2,1,0:T(8,128)(2,1)S(1)}, u32[]{:S(2)}, u32[]{:S(2)}) collective-permute-start(bf16[12,64,128]{2,1,0:T(8,128)(2,1)S(1)} %collective-permute-done.4.refs_6_), channel_id=1, source_target_pairs={{0,192},{64,0},{128,64},{192,128},{1,193},{65,1},{129,65},{193,129... | collective-permute-start | bytes 589832 | tf_op jit(solution)/shard_map/ppermute | solution.py:258
  33.4 1.6 %collective-permute-done.3.refs_5_ = bf16[12,64,128]{2,1,0:T(8,128)(2,1)S(1)} collective-permute-done((bf16[12,64,128]{2,1,0:T(8,128)(2,1)S(1)}, bf16[12,64,128]{2,1,0:T(8,128)(2,1)S(1)}, u32[]{:S(2)}, u32[]{:S(2)}) %collective-permute-start.3) | collective-permute-done | bytes 196640 | tf_op jit(solution)/shard_map/ppermute | solution.py:255
  34.9 3.4 %collective-permute-done.2.refs_3_ = bf16[12,64,128]{2,1,0:T(8,128)(2,1)S(1)} collective-permute-done((bf16[12,64,128]{2,1,0:T(8,128)(2,1)S(1)}, bf16[12,64,128]{2,1,0:T(8,128)(2,1)S(1)}, u32[]{:S(2)}, u32[]{:S(2)}) %collective-permute-start.2) | collective-permute-done | bytes 196640 | tf_op jit(solution)/shard_map/ppermute | solution.py:257
  41.1 2.6 %shard_map.78 = (bf16[33,2,64,128]{3,2,1,0:T(8,128)(2,1)}, bf16[33,2,64,128]{3,2,1,0:T(8,128)(2,1)S(1)}) custom-call(s32[1,24]{1,0:T(1,128)S(1)} %copy-done.8, s32[8,4]{1,0:T(8,128)S(1)} %copy.8.cos_ref, bf16[2,128,128]{2,1,0:T(8,128)(2,1)S(1)} %get-tuple-element.24.metric_ref, bf16[12,64,128]{2,1,0:T(8,128)(2,1)S(1)} %copy-done.1, ...), custom_call_target="tpu_custom_call" | custom-call | flops 1000000000 | bytes 1638624 | tf_op jit(solution)/shard_map/pallas_call | solution.py:46
  44.0 1.6 %collective-permute-start.24 = (bf16[8,2,64,128]{3,2,1,0:T(8,128)(2,1)S(1)}, bf16[8,2,64,128]{3,2,1,0:T(8,128)(2,1)S(1)}, u32[]{:S(2)}, u32[]{:S(2)}) collective-permute-start(bf16[8,2,64,128]{3,2,1,0:T(8,128)(2,1)S(1)} %get-tuple-element.42), channel_id=1, source_target_pairs={{0,16},{1,17},{2,18},{3,19},{4,20},{5,21},{6,22},{7,23},{8,24},{9,... | collective-permute-start | bytes 786440 | tf_op jit(solution)/shard_map/ppermute | solution.py:274
  45.5 2.3 %collective-permute-start.25 = (bf16[8,2,64,128]{3,2,1,0:T(8,128)(2,1)S(1)}, bf16[8,2,64,128]{3,2,1,0:T(8,128)(2,1)S(1)}, u32[]{:S(2)}, u32[]{:S(2)}) collective-permute-start(bf16[8,2,64,128]{3,2,1,0:T(8,128)(2,1)S(1)} %get-tuple-element.43), channel_id=1, source_target_pairs={{0,32},{1,33},{2,34},{3,35},{4,36},{5,37},{6,38},{7,39},{8,40},{9,... | collective-permute-start | bytes 786440 | tf_op jit(solution)/shard_map/ppermute | solution.py:274
  48.8 4.4 %collective-permute-done.24.b_ref = bf16[8,2,64,128]{3,2,1,0:T(8,128)(2,1)S(1)} collective-permute-done((bf16[8,2,64,128]{3,2,1,0:T(8,128)(2,1)S(1)}, bf16[8,2,64,128]{3,2,1,0:T(8,128)(2,1)S(1)}, u32[]{:S(2)}, u32[]{:S(2)}) %collective-permute-start.24) | collective-permute-done | bytes 262176 | tf_op jit(solution)/shard_map/ppermute | solution.py:274
  53.2 3.0 %collective-permute-done.25.c_ref = bf16[8,2,64,128]{3,2,1,0:T(8,128)(2,1)S(1)} collective-permute-done((bf16[8,2,64,128]{3,2,1,0:T(8,128)(2,1)S(1)}, bf16[8,2,64,128]{3,2,1,0:T(8,128)(2,1)S(1)}, u32[]{:S(2)}, u32[]{:S(2)}) %collective-permute-start.25) | collective-permute-done | bytes 262176 | tf_op jit(solution)/shard_map/ppermute | solution.py:274
  56.3 4.8 %collective-permute-done.26.d_ref = bf16[8,2,64,128]{3,2,1,0:T(8,128)(2,1)S(1)} collective-permute-done((bf16[8,2,64,128]{3,2,1,0:T(8,128)(2,1)S(1)}, bf16[8,2,64,128]{3,2,1,0:T(8,128)(2,1)S(1)}, u32[]{:S(2)}, u32[]{:S(2)}) %collective-permute-start.26) | collective-permute-done | bytes 262176 | tf_op jit(solution)/shard_map/ppermute | solution.py:274
  61.9 7.8 %all-to-all-start = ((bf16[8,2,64,128]{3,2,1,0:T(8,128)(2,1)}), bf16[8,2,64,128]{3,2,1,0:T(8,128)(2,1)S(1)}, u32[]{:S(2)}, u32[]{:S(2)}) async-start(bf16[8,2,64,128]{3,2,1,0:T(8,128)(2,1)} %shard_map.84), calls=%async_computation | async-start | bytes 524288 | tf_op jit(solution)/shard_map/all_to_all | solution.py:238
  74.1 1.7 %collective-permute-start.9 = (bf16[8,2,64,128]{3,2,1,0:T(8,128)(2,1)S(1)}, bf16[8,2,64,128]{3,2,1,0:T(8,128)(2,1)S(1)}, u32[]{:S(2)}, u32[]{:S(2)}) collective-permute-start(bf16[8,2,64,128]{3,2,1,0:T(8,128)(2,1)S(1)} %get-tuple-element.30), channel_id=1, source_target_pairs={{0,48},{1,49},{2,50},{3,51},{4,52},{5,53},{6,54},{7,55},{8,56},{9,... | collective-permute-start | bytes 786440 | tf_op jit(solution)/shard_map/ppermute | solution.py:274
  75.8 4.8 %collective-permute-done.7.b_ref = bf16[8,2,64,128]{3,2,1,0:T(8,128)(2,1)S(1)} collective-permute-done((bf16[8,2,64,128]{3,2,1,0:T(8,128)(2,1)S(1)}, bf16[8,2,64,128]{3,2,1,0:T(8,128)(2,1)S(1)}, u32[]{:S(2)}, u32[]{:S(2)}) %collective-permute-start.7) | collective-permute-done | bytes 262176 | tf_op jit(solution)/shard_map/ppermute | solution.py:274
  80.5 2.8 %collective-permute-done.8.c_ref = bf16[8,2,64,128]{3,2,1,0:T(8,128)(2,1)S(1)} collective-permute-done((bf16[8,2,64,128]{3,2,1,0:T(8,128)(2,1)S(1)}, bf16[8,2,64,128]{3,2,1,0:T(8,128)(2,1)S(1)}, u32[]{:S(2)}, u32[]{:S(2)}) %collective-permute-start.8) | collective-permute-done | bytes 262176 | tf_op jit(solution)/shard_map/ppermute | solution.py:274
  83.3 3.4 %collective-permute-done.9.d_ref = bf16[8,2,64,128]{3,2,1,0:T(8,128)(2,1)S(1)} collective-permute-done((bf16[8,2,64,128]{3,2,1,0:T(8,128)(2,1)S(1)}, bf16[8,2,64,128]{3,2,1,0:T(8,128)(2,1)S(1)}, u32[]{:S(2)}, u32[]{:S(2)}) %collective-permute-start.9) | collective-permute-done | bytes 262176 | tf_op jit(solution)/shard_map/ppermute | solution.py:274
  86.9 1.8 %collective-permute-start.10 = (bf16[2,64,128]{2,1,0:T(8,128)(2,1)S(1)}, bf16[2,64,128]{2,1,0:T(8,128)(2,1)S(1)}, u32[]{:S(2)}, u32[]{:S(2)}) collective-permute-start(bf16[2,64,128]{2,1,0:T(8,128)(2,1)S(1)} %get-tuple-element.32), channel_id=1, source_target_pairs={{0,2},{1,3},{2,4},{3,5},{4,6},{5,7},{6,8},{7,9},{8,10},{9,11},{10,... | collective-permute-start | bytes 98312 | tf_op jit(solution)/shard_map/ppermute | solution.py:277
  88.7 2.4 %collective-permute-start.11 = (bf16[2,64,128]{2,1,0:T(8,128)(2,1)S(1)}, bf16[2,64,128]{2,1,0:T(8,128)(2,1)S(1)}, u32[]{:S(2)}, u32[]{:S(2)}) collective-permute-start(bf16[2,64,128]{2,1,0:T(8,128)(2,1)S(1)} %get-tuple-element.33), channel_id=1, source_target_pairs={{0,4},{1,5},{2,6},{3,7},{4,8},{5,9},{6,10},{7,11},{8,12},{9,13},{1... | collective-permute-start | bytes 98312 | tf_op jit(solution)/shard_map/ppermute | solution.py:277
  91.0 2.7 %collective-permute-start.12 = (bf16[2,64,128]{2,1,0:T(8,128)(2,1)S(1)}, bf16[2,64,128]{2,1,0:T(8,128)(2,1)S(1)}, u32[]{:S(2)}, u32[]{:S(2)}) collective-permute-start(bf16[2,64,128]{2,1,0:T(8,128)(2,1)S(1)} %get-tuple-element.34), channel_id=1, source_target_pairs={{0,6},{1,7},{2,8},{3,9},{4,10},{5,11},{6,12},{7,13},{8,14},{9,15},... | collective-permute-start | bytes 98312 | tf_op jit(solution)/shard_map/ppermute | solution.py:277
  93.7 2.4 %collective-permute-start.13 = (bf16[2,64,128]{2,1,0:T(8,128)(2,1)S(1)}, bf16[2,64,128]{2,1,0:T(8,128)(2,1)S(1)}, u32[]{:S(2)}, u32[]{:S(2)}) collective-permute-start(bf16[2,64,128]{2,1,0:T(8,128)(2,1)S(1)} %get-tuple-element.35), channel_id=1, source_target_pairs={{0,8},{1,9},{2,10},{3,11},{4,12},{5,13},{6,14},{7,15},{8,0},{9,1},... | collective-permute-start | bytes 98312 | tf_op jit(solution)/shard_map/ppermute | solution.py:277
  96.1 2.7 %collective-permute-start.14 = (bf16[2,64,128]{2,1,0:T(8,128)(2,1)S(1)}, bf16[2,64,128]{2,1,0:T(8,128)(2,1)S(1)}, u32[]{:S(2)}, u32[]{:S(2)}) collective-permute-start(bf16[2,64,128]{2,1,0:T(8,128)(2,1)S(1)} %get-tuple-element.36), channel_id=1, source_target_pairs={{0,10},{1,11},{2,12},{3,13},{4,14},{5,15},{6,0},{7,1},{8,2},{9,3},... | collective-permute-start | bytes 98312 | tf_op jit(solution)/shard_map/ppermute | solution.py:277
  98.8 3.6 %collective-permute-start.15 = (bf16[2,64,128]{2,1,0:T(8,128)(2,1)S(1)}, bf16[2,64,128]{2,1,0:T(8,128)(2,1)S(1)}, u32[]{:S(2)}, u32[]{:S(2)}) collective-permute-start(bf16[2,64,128]{2,1,0:T(8,128)(2,1)S(1)} %get-tuple-element.37), channel_id=1, source_target_pairs={{0,12},{1,13},{2,14},{3,15},{4,0},{5,1},{6,2},{7,3},{8,4},{9,5},{1... | collective-permute-start | bytes 98312 | tf_op jit(solution)/shard_map/ppermute | solution.py:277
  104.3 2.0 %collective-permute-done.16.refs_7_ = bf16[2,64,128]{2,1,0:T(8,128)(2,1)S(1)} collective-permute-done((bf16[2,64,128]{2,1,0:T(8,128)(2,1)S(1)}, bf16[2,64,128]{2,1,0:T(8,128)(2,1)S(1)}, u32[]{:S(2)}, u32[]{:S(2)}) %collective-permute-start.16) | collective-permute-done | bytes 32800 | tf_op jit(solution)/shard_map/ppermute | solution.py:277
  107.1 1.8 %collective-permute-start.28 = (bf16[128,128]{1,0:T(8,128)(2,1)S(1)}, bf16[128,128]{1,0:T(8,128)(2,1)S(1)}, u32[]{:S(2)}, u32[]{:S(2)}) collective-permute-start(bf16[128,128]{1,0:T(8,128)(2,1)S(1)} %shard_map.86.a_ref), channel_id=1, source_target_pairs={{0,128},{64,192},{128,0},{192,64},{1,129},{65,193},{129,1},{193,65... | collective-permute-start | bytes 98312 | tf_op jit(solution)/shard_map/ppermute | solution.py:284
  110.1 3.4 %final.1 = bf16[2,128,2,2048]{3,2,1,0:T(2,128)(2,1)} custom-call(bf16[128,4096]{1,0:T(8,128)(2,1)S(1)} %bitcast.15, bf16[128,4096]{1,0:T(8,128)(2,1)S(1)} %bitcast.16, bf16[128,4096]{1,0:T(8,128)(2,1)S(1)} %bitcast.18, bf16[128,4096]{1,0:T(8,128)(2,1)S(1)} %bitcast.19, f32[2,4096]{1,0:T(2,128)S(1)} %bitcast.21, f32[2,4096]{1,0:T(2,128)S(1)} %bitcast.22, ...), custom_call_target="tpu_custom_call" | custom-call | flops 1000000000 | bytes 4194304 | tf_op jit(solution)/shard_map/final/pallas_call | solution.py:205
  (77 shorter events, 23.6 us)
Async XLA Ops:
  2.0 8.2 %collective-permute-start.17 = (bf16[12,64,128]{2,1,0:T(8,128)(2,1)S(1)}, bf16[12,64,128]{2,1,0:T(8,128)(2,1)}, u32[]{:S(2)}, u32[]{:S(2)}) collective-permute-start(bf16[12,64,128]{2,1,0:T(8,128)(2,1)S(1)} %get-tuple-element.49.refs_0_), channel_id=1, source_target_pairs={{0,64},{64,128},{128,192},{192,0},{1,65},{65,129},{129,193},{193,1... | collective-permute-start | bytes 589832 | tf_op jit(solution)/shard_map/ppermute | solution.py:253
  3.7 7.9 %collective-permute-start.21 = (bf16[12,64,128]{2,1,0:T(8,128)(2,1)S(1)}, bf16[12,64,128]{2,1,0:T(8,128)(2,1)}, u32[]{:S(2)}, u32[]{:S(2)}) collective-permute-start(bf16[12,64,128]{2,1,0:T(8,128)(2,1)S(1)} %get-tuple-element.46.refs_4_), channel_id=1, source_target_pairs={{0,192},{64,0},{128,64},{192,128},{1,193},{65,1},{129,65},{193,129... | collective-permute-start | bytes 589832 | tf_op jit(solution)/shard_map/ppermute | solution.py:254
  5.3 10.3 %collective-permute-start.18 = (bf16[12,64,128]{2,1,0:T(8,128)(2,1)S(1)}, bf16[12,64,128]{2,1,0:T(8,128)(2,1)S(1)}, u32[]{:S(2)}, u32[]{:S(2)}) collective-permute-start(bf16[12,64,128]{2,1,0:T(8,128)(2,1)S(1)} %get-tuple-element.49.refs_0_), channel_id=1, source_target_pairs={{0,192},{64,0},{128,64},{192,128},{1,193},{65,1},{129,65},{193,129... | collective-permute-start | bytes 589832 | tf_op jit(solution)/shard_map/ppermute | solution.py:256
  7.1 15.0 %collective-permute-start.20 = (bf16[12,64,128]{2,1,0:T(8,128)(2,1)S(1)}, bf16[12,64,128]{2,1,0:T(8,128)(2,1)}, u32[]{:S(2)}, u32[]{:S(2)}) collective-permute-start(bf16[12,64,128]{2,1,0:T(8,128)(2,1)S(1)} %get-tuple-element.46.refs_4_), channel_id=1, source_target_pairs={{0,64},{64,128},{128,192},{192,0},{1,65},{65,129},{129,193},{193,1... | collective-permute-start | bytes 589832 | tf_op jit(solution)/shard_map/ppermute | solution.py:255
  10.2 11.9 %collective-permute-start.19 = (bf16[12,64,128]{2,1,0:T(8,128)(2,1)}, bf16[12,64,128]{2,1,0:T(8,128)(2,1)}, u32[]{:S(2)}, u32[]{:S(2)}) collective-permute-start(bf16[12,64,128]{2,1,0:T(8,128)(2,1)} %collective-permute-done.17.refs_1_), channel_id=1, source_target_pairs={{0,64},{64,128},{128,192},{192,0},{1,65},{65,129},{129,193},{193,1... | collective-permute-start | bytes 589832 | tf_op jit(solution)/shard_map/ppermute | solution.py:257
  11.6 10.6 %collective-permute-start.22 = (bf16[12,64,128]{2,1,0:T(8,128)(2,1)}, bf16[12,64,128]{2,1,0:T(8,128)(2,1)}, u32[]{:S(2)}, u32[]{:S(2)}) collective-permute-start(bf16[12,64,128]{2,1,0:T(8,128)(2,1)} %collective-permute-done.21.refs_6_), channel_id=1, source_target_pairs={{0,192},{64,0},{128,64},{192,128},{1,193},{65,1},{129,65},{193,129... | collective-permute-start | bytes 589832 | tf_op jit(solution)/shard_map/ppermute | solution.py:258
  14.4 13.2 %collective-permute-start = (bf16[12,64,128]{2,1,0:T(8,128)(2,1)S(1)}, bf16[12,64,128]{2,1,0:T(8,128)(2,1)S(1)}, u32[]{:S(2)}, u32[]{:S(2)}) collective-permute-start(bf16[12,64,128]{2,1,0:T(8,128)(2,1)S(1)} %get-tuple-element.48.refs_0_), channel_id=1, source_target_pairs={{0,64},{64,128},{128,192},{192,0},{1,65},{65,129},{129,193},{193,1... | collective-permute-start | bytes 589832 | tf_op jit(solution)/shard_map/ppermute | solution.py:253
  16.3 12.0 %collective-permute-start.4 = (bf16[12,64,128]{2,1,0:T(8,128)(2,1)S(1)}, bf16[12,64,128]{2,1,0:T(8,128)(2,1)S(1)}, u32[]{:S(2)}, u32[]{:S(2)}) collective-permute-start(bf16[12,64,128]{2,1,0:T(8,128)(2,1)S(1)} %get-tuple-element.47.refs_4_), channel_id=1, source_target_pairs={{0,192},{64,0},{128,64},{192,128},{1,193},{65,1},{129,65},{193,129... | collective-permute-start | bytes 589832 | tf_op jit(solution)/shard_map/ppermute | solution.py:254
  25.4 18.3 %collective-permute-start.23 = (bf16[33,2,64,128]{3,2,1,0:T(8,128)(2,1)S(1)}, bf16[33,2,64,128]{3,2,1,0:T(8,128)(2,1)S(1)}, u32[]{:S(2)}, u32[]{:S(2)}) collective-permute-start(bf16[33,2,64,128]{3,2,1,0:T(8,128)(2,1)S(1)} %get-tuple-element.40), channel_id=1, source_target_pairs={{0,1},{1,0},{2,3},{3,2},{4,5},{5,4},{6,7},{7,6},{8,9},{9,8},{10,11... | collective-permute-start | bytes 3244040 | tf_op jit(solution)/shard_map/ppermute | solution.py:272
  25.5 7.8 %collective-permute-start.1 = (bf16[12,64,128]{2,1,0:T(8,128)(2,1)S(1)}, bf16[12,64,128]{2,1,0:T(8,128)(2,1)S(1)}, u32[]{:S(2)}, u32[]{:S(2)}) collective-permute-start(bf16[12,64,128]{2,1,0:T(8,128)(2,1)S(1)} %get-tuple-element.48.refs_0_), channel_id=1, source_target_pairs={{0,192},{64,0},{128,64},{192,128},{1,193},{65,1},{129,65},{193,129... | collective-permute-start | bytes 589832 | tf_op jit(solution)/shard_map/ppermute | solution.py:256
  26.0 9.0 %collective-permute-start.3 = (bf16[12,64,128]{2,1,0:T(8,128)(2,1)S(1)}, bf16[12,64,128]{2,1,0:T(8,128)(2,1)S(1)}, u32[]{:S(2)}, u32[]{:S(2)}) collective-permute-start(bf16[12,64,128]{2,1,0:T(8,128)(2,1)S(1)} %get-tuple-element.47.refs_4_), channel_id=1, source_target_pairs={{0,64},{64,128},{128,192},{192,0},{1,65},{65,129},{129,193},{193,1... | collective-permute-start | bytes 589832 | tf_op jit(solution)/shard_map/ppermute | solution.py:255
  27.6 10.7 %collective-permute-start.2 = (bf16[12,64,128]{2,1,0:T(8,128)(2,1)S(1)}, bf16[12,64,128]{2,1,0:T(8,128)(2,1)S(1)}, u32[]{:S(2)}, u32[]{:S(2)}) collective-permute-start(bf16[12,64,128]{2,1,0:T(8,128)(2,1)S(1)} %collective-permute-done.refs_1_), channel_id=1, source_target_pairs={{0,64},{64,128},{128,192},{192,0},{1,65},{65,129},{129,193},{193,1... | collective-permute-start | bytes 589832 | tf_op jit(solution)/shard_map/ppermute | solution.py:257
  28.3 10.0 %collective-permute-start.5 = (bf16[12,64,128]{2,1,0:T(8,128)(2,1)S(1)}, bf16[12,64,128]{2,1,0:T(8,128)(2,1)S(1)}, u32[]{:S(2)}, u32[]{:S(2)}) collective-permute-start(bf16[12,64,128]{2,1,0:T(8,128)(2,1)S(1)} %collective-permute-done.4.refs_6_), channel_id=1, source_target_pairs={{0,192},{64,0},{128,64},{192,128},{1,193},{65,1},{129,65},{193,129... | collective-permute-start | bytes 589832 | tf_op jit(solution)/shard_map/ppermute | solution.py:258
  43.7 26.0 %collective-permute-start.6 = (bf16[33,2,64,128]{3,2,1,0:T(8,128)(2,1)}, bf16[33,2,64,128]{3,2,1,0:T(8,128)(2,1)}, u32[]{:S(2)}, u32[]{:S(2)}) collective-permute-start(bf16[33,2,64,128]{3,2,1,0:T(8,128)(2,1)} %get-tuple-element.26), channel_id=1, source_target_pairs={{0,1},{1,0},{2,3},{3,2},{4,5},{5,4},{6,7},{7,6},{8,9},{9,8},{10,11... | collective-permute-start | bytes 3244040 | tf_op jit(solution)/shard_map/ppermute | solution.py:272
  44.0 9.3 %collective-permute-start.24 = (bf16[8,2,64,128]{3,2,1,0:T(8,128)(2,1)S(1)}, bf16[8,2,64,128]{3,2,1,0:T(8,128)(2,1)S(1)}, u32[]{:S(2)}, u32[]{:S(2)}) collective-permute-start(bf16[8,2,64,128]{3,2,1,0:T(8,128)(2,1)S(1)} %get-tuple-element.42), channel_id=1, source_target_pairs={{0,16},{1,17},{2,18},{3,19},{4,20},{5,21},{6,22},{7,23},{8,24},{9,... | collective-permute-start | bytes 786440 | tf_op jit(solution)/shard_map/ppermute | solution.py:274
  45.5 10.7 %collective-permute-start.25 = (bf16[8,2,64,128]{3,2,1,0:T(8,128)(2,1)S(1)}, bf16[8,2,64,128]{3,2,1,0:T(8,128)(2,1)S(1)}, u32[]{:S(2)}, u32[]{:S(2)}) collective-permute-start(bf16[8,2,64,128]{3,2,1,0:T(8,128)(2,1)S(1)} %get-tuple-element.43), channel_id=1, source_target_pairs={{0,32},{1,33},{2,34},{3,35},{4,36},{5,37},{6,38},{7,39},{8,40},{9,... | collective-permute-start | bytes 786440 | tf_op jit(solution)/shard_map/ppermute | solution.py:274
  47.8 13.3 %collective-permute-start.26 = (bf16[8,2,64,128]{3,2,1,0:T(8,128)(2,1)S(1)}, bf16[8,2,64,128]{3,2,1,0:T(8,128)(2,1)S(1)}, u32[]{:S(2)}, u32[]{:S(2)}) collective-permute-start(bf16[8,2,64,128]{3,2,1,0:T(8,128)(2,1)S(1)} %get-tuple-element.44), channel_id=1, source_target_pairs={{0,48},{1,49},{2,50},{3,51},{4,52},{5,53},{6,54},{7,55},{8,56},{9,... | collective-permute-start | bytes 786440 | tf_op jit(solution)/shard_map/ppermute | solution.py:274
  61.9 44.4 %all-to-all-start = ((bf16[8,2,64,128]{3,2,1,0:T(8,128)(2,1)}), bf16[8,2,64,128]{3,2,1,0:T(8,128)(2,1)S(1)}, u32[]{:S(2)}, u32[]{:S(2)}) async-start(bf16[8,2,64,128]{3,2,1,0:T(8,128)(2,1)} %shard_map.84), calls=%async_computation | async-start | bytes 524288 | tf_op jit(solution)/shard_map/all_to_all | solution.py:238
  71.2 35.1 %copy-start.10 = (bf16[2,2,128,256]{3,2,1,0:T(8,128)(2,1)S(1)}, bf16[2,2,128,256]{3,2,1,0:T(8,128)(2,1)}, u32[]{:S(2)}) copy-start(bf16[2,2,128,256]{3,2,1,0:T(8,128)(2,1)} %copy-done.9) | copy-start | bytes 786436
  71.3 9.3 %collective-permute-start.7 = (bf16[8,2,64,128]{3,2,1,0:T(8,128)(2,1)S(1)}, bf16[8,2,64,128]{3,2,1,0:T(8,128)(2,1)S(1)}, u32[]{:S(2)}, u32[]{:S(2)}) collective-permute-start(bf16[8,2,64,128]{3,2,1,0:T(8,128)(2,1)S(1)} %get-tuple-element.28), channel_id=1, source_target_pairs={{0,16},{1,17},{2,18},{3,19},{4,20},{5,21},{6,22},{7,23},{8,24},{9,... | collective-permute-start | bytes 786440 | tf_op jit(solution)/shard_map/ppermute | solution.py:274
  72.6 10.7 %collective-permute-start.8 = (bf16[8,2,64,128]{3,2,1,0:T(8,128)(2,1)S(1)}, bf16[8,2,64,128]{3,2,1,0:T(8,128)(2,1)S(1)}, u32[]{:S(2)}, u32[]{:S(2)}) collective-permute-start(bf16[8,2,64,128]{3,2,1,0:T(8,128)(2,1)S(1)} %get-tuple-element.29), channel_id=1, source_target_pairs={{0,32},{1,33},{2,34},{3,35},{4,36},{5,37},{6,38},{7,39},{8,40},{9,... | collective-permute-start | bytes 786440 | tf_op jit(solution)/shard_map/ppermute | solution.py:274
  74.1 12.6 %collective-permute-start.9 = (bf16[8,2,64,128]{3,2,1,0:T(8,128)(2,1)S(1)}, bf16[8,2,64,128]{3,2,1,0:T(8,128)(2,1)S(1)}, u32[]{:S(2)}, u32[]{:S(2)}) collective-permute-start(bf16[8,2,64,128]{3,2,1,0:T(8,128)(2,1)S(1)} %get-tuple-element.30), channel_id=1, source_target_pairs={{0,48},{1,49},{2,50},{3,51},{4,52},{5,53},{6,54},{7,55},{8,56},{9,... | collective-permute-start | bytes 786440 | tf_op jit(solution)/shard_map/ppermute | solution.py:274
  86.9 11.9 %collective-permute-start.10 = (bf16[2,64,128]{2,1,0:T(8,128)(2,1)S(1)}, bf16[2,64,128]{2,1,0:T(8,128)(2,1)S(1)}, u32[]{:S(2)}, u32[]{:S(2)}) collective-permute-start(bf16[2,64,128]{2,1,0:T(8,128)(2,1)S(1)} %get-tuple-element.32), channel_id=1, source_target_pairs={{0,2},{1,3},{2,4},{3,5},{4,6},{5,7},{6,8},{7,9},{8,10},{9,11},{10,... | collective-permute-start | bytes 98312 | tf_op jit(solution)/shard_map/ppermute | solution.py:277
  88.7 13.7 %collective-permute-start.11 = (bf16[2,64,128]{2,1,0:T(8,128)(2,1)S(1)}, bf16[2,64,128]{2,1,0:T(8,128)(2,1)S(1)}, u32[]{:S(2)}, u32[]{:S(2)}) collective-permute-start(bf16[2,64,128]{2,1,0:T(8,128)(2,1)S(1)} %get-tuple-element.33), channel_id=1, source_target_pairs={{0,4},{1,5},{2,6},{3,7},{4,8},{5,9},{6,10},{7,11},{8,12},{9,13},{1... | collective-permute-start | bytes 98312 | tf_op jit(solution)/shard_map/ppermute | solution.py:277
  91.0 12.8 %collective-permute-start.12 = (bf16[2,64,128]{2,1,0:T(8,128)(2,1)S(1)}, bf16[2,64,128]{2,1,0:T(8,128)(2,1)S(1)}, u32[]{:S(2)}, u32[]{:S(2)}) collective-permute-start(bf16[2,64,128]{2,1,0:T(8,128)(2,1)S(1)} %get-tuple-element.34), channel_id=1, source_target_pairs={{0,6},{1,7},{2,8},{3,9},{4,10},{5,11},{6,12},{7,13},{8,14},{9,15},... | collective-permute-start | bytes 98312 | tf_op jit(solution)/shard_map/ppermute | solution.py:277
  93.7 10.1 %collective-permute-start.13 = (bf16[2,64,128]{2,1,0:T(8,128)(2,1)S(1)}, bf16[2,64,128]{2,1,0:T(8,128)(2,1)S(1)}, u32[]{:S(2)}, u32[]{:S(2)}) collective-permute-start(bf16[2,64,128]{2,1,0:T(8,128)(2,1)S(1)} %get-tuple-element.35), channel_id=1, source_target_pairs={{0,8},{1,9},{2,10},{3,11},{4,12},{5,13},{6,14},{7,15},{8,0},{9,1},... | collective-permute-start | bytes 98312 | tf_op jit(solution)/shard_map/ppermute | solution.py:277
  96.1 7.7 %collective-permute-start.14 = (bf16[2,64,128]{2,1,0:T(8,128)(2,1)S(1)}, bf16[2,64,128]{2,1,0:T(8,128)(2,1)S(1)}, u32[]{:S(2)}, u32[]{:S(2)}) collective-permute-start(bf16[2,64,128]{2,1,0:T(8,128)(2,1)S(1)} %get-tuple-element.36), channel_id=1, source_target_pairs={{0,10},{1,11},{2,12},{3,13},{4,14},{5,15},{6,0},{7,1},{8,2},{9,3},... | collective-permute-start | bytes 98312 | tf_op jit(solution)/shard_map/ppermute | solution.py:277
  98.8 5.5 %collective-permute-start.15 = (bf16[2,64,128]{2,1,0:T(8,128)(2,1)S(1)}, bf16[2,64,128]{2,1,0:T(8,128)(2,1)S(1)}, u32[]{:S(2)}, u32[]{:S(2)}) collective-permute-start(bf16[2,64,128]{2,1,0:T(8,128)(2,1)S(1)} %get-tuple-element.37), channel_id=1, source_target_pairs={{0,12},{1,13},{2,14},{3,15},{4,0},{5,1},{6,2},{7,3},{8,4},{9,5},{1... | collective-permute-start | bytes 98312 | tf_op jit(solution)/shard_map/ppermute | solution.py:277
  102.3 3.9 %collective-permute-start.16 = (bf16[2,64,128]{2,1,0:T(8,128)(2,1)S(1)}, bf16[2,64,128]{2,1,0:T(8,128)(2,1)S(1)}, u32[]{:S(2)}, u32[]{:S(2)}) collective-permute-start(bf16[2,64,128]{2,1,0:T(8,128)(2,1)S(1)} %get-tuple-element.38), channel_id=1, source_target_pairs={{0,14},{1,15},{2,0},{3,1},{4,2},{5,3},{6,4},{7,5},{8,6},{9,7},{10,... | collective-permute-start | bytes 98312 | tf_op jit(solution)/shard_map/ppermute | solution.py:277
  106.6 6.9 %collective-permute-start.27 = (bf16[128,128]{1,0:T(8,128)(2,1)S(1)}, bf16[128,128]{1,0:T(8,128)(2,1)S(1)}, u32[]{:S(2)}, u32[]{:S(2)}) collective-permute-start(bf16[128,128]{1,0:T(8,128)(2,1)S(1)} %shard_map.86.a_ref), channel_id=1, source_target_pairs={{0,64},{64,128},{128,192},{192,0},{1,65},{65,129},{129,193},{193,1... | collective-permute-start | bytes 98312 | tf_op jit(solution)/shard_map/ppermute | solution.py:284
  107.1 6.4 %collective-permute-start.28 = (bf16[128,128]{1,0:T(8,128)(2,1)S(1)}, bf16[128,128]{1,0:T(8,128)(2,1)S(1)}, u32[]{:S(2)}, u32[]{:S(2)}) collective-permute-start(bf16[128,128]{1,0:T(8,128)(2,1)S(1)} %shard_map.86.a_ref), channel_id=1, source_target_pairs={{0,128},{64,192},{128,0},{192,64},{1,129},{65,193},{129,1},{193,65... | collective-permute-start | bytes 98312 | tf_op jit(solution)/shard_map/ppermute | solution.py:284
  108.9 4.6 %collective-permute-start.29 = (bf16[128,128]{1,0:T(8,128)(2,1)S(1)}, bf16[128,128]{1,0:T(8,128)(2,1)S(1)}, u32[]{:S(2)}, u32[]{:S(2)}) collective-permute-start(bf16[128,128]{1,0:T(8,128)(2,1)S(1)} %shard_map.86.a_ref), channel_id=1, source_target_pairs={{0,192},{64,0},{128,64},{192,128},{1,193},{65,1},{129,65},{193,129... | collective-permute-start | bytes 98312 | tf_op jit(solution)/shard_map/ppermute | solution.py:284
  (14 other events, 62.5 us)
where the time goes:
time: 115 us; the launch traced here: 114 us
  starting transfers between devices  55.7 us (48%)
  waiting for transfers between devices  34.8 us (30%)
  Pallas kernels  13.8 us (12%)
  local copies, waits for them, and re-layouts  9.03 us (8%)
    ppermute x6, waiting for transfers between devices, work(): moved = [lax.ppermute(both[d], 'blk', x_shift(d)) for d in range(1, NX)]  23.3 us
    ppermute x7, starting transfers between devices, work(): moved = [lax.ppermute(both[d], 'blk', z_shift(d)) for d in range(1, NZ)]  16.9 us
    pallas_call x11, Pallas kernels, call(): pl.pallas_call(body, out_shape=out_shape, in_specs=[pl.BlockSpec(memory_s...  10.4 us
    ppermute x6, starting transfers between devices, work(): moved = [lax.ppermute(both[d], 'blk', x_shift(d)) for d in range(1, NX)]  9.33 us
    all_to_all x1, starting transfers between devices, exchange(): lax.all_to_all(value, 'blk', 0, 0, axis_index_groups=groups, tiled=True)  7.79 us
    unnamed x34, local copies, waits for them, and re-layouts  7.67 us
    ppermute x2, starting transfers between devices, work(): far_b = lax.ppermute(high_b, 'tm', down)  6.08 us
    ppermute x2, starting transfers between devices, work(): high_b = lax.ppermute(mine[1], 'tm', down)  4.84 us
  transfers between devices with their start and end apart: 31, of which 13 were waited for; matrix products, arithmetic and copies ran while one was open for 1% of the time, Pallas kernels for 11%

commit v1 on v0

--- a/solution.py
+++ b/solution.py
@@ -9,7 +9,6 @@
 
 
 CHUNKS = (64, 64)
-LAST_BY_GROUP = True
 NX, NZ, NC, NY = 4, 8, 2, 4
 
 bf16 = jnp.bfloat16
@@ -29,10 +28,6 @@
 
 def x_shift(d):
     return [(blk_of(x, z, c), blk_of((x + d) % NX, z, c)) for x, z in CHIPS for c in range(NC)]
-
-
-def z_shift(d):
-    return [(blk_of(x, z, c), blk_of(x, (z + d) % NZ, c)) for x, z in CHIPS for c in range(NC)]
 
 
 def y_shift(d):
@@ -123,14 +118,6 @@
         lax.fori_loop(0, NZ, body, 0, unroll=4)
 
 
-def sum_split_body(a_ref, b_ref, c_ref, d_ref, *out_refs):
-    my_z = (lax.axis_index("blk") >> 1) & 7
-    for d, out_ref in enumerate(out_refs):
-        i = (my_z + d) & 7
-        low = a_ref[i].astype(f32) + b_ref[i].astype(f32)
-        out_ref[...] = (low + (c_ref[i].astype(f32) + d_ref[i].astype(f32))).astype(bf16)
-
-
 def sum_body(a_ref, b_ref, c_ref, d_ref, out_ref):
     def body(i, _):
         low = a_ref[i].astype(f32) + b_ref[i].astype(f32)
@@ -138,13 +125,6 @@
         return 0
 
     lax.fori_loop(0, NZ, body, 0, unroll=4)
-
-
-def sum_all_body(*refs):
-    total = refs[0][...].astype(f32)
-    for r in refs[1:-1]:
-        total = total + r[...].astype(f32)
-    refs[-1][...] = total.astype(bf16)
 
 
 def sum_lead_body(in_ref, out_ref):
@@ -272,14 +252,9 @@
         other = lax.ppermute(send, "blk", CORE_SWAP)
         both = call(add_split_body, [piece] * NX, keep, other, flops=10**7)
         moved = [lax.ppermute(both[d], "blk", x_shift(d)) for d in range(1, NX)]
-        if c == 0 or not LAST_BY_GROUP:
-            both = call(sum_split_body, [small] * NZ, both[0], *moved, flops=10**7)
-            moved = [lax.ppermute(both[d], "blk", z_shift(d)) for d in range(1, NZ)]
-            collected.append(call(sum_all_body, small, both[0], *moved, flops=10**7))
-        else:
-            both = call(sum_body, piece, both[0], *moved, flops=10**7)
-            both = exchange(both, Z_GROUPS)
-            collected.append(call(sum_lead_body, small, both, flops=10**7))
+        both = call(sum_body, piece, both[0], *moved, flops=10**7)
+        both = exchange(both, Z_GROUPS)
+        collected.append(call(sum_lead_body, small, both, flops=10**7))
     dpart = call(density_body, sds((block, block)), gram, *collected, flops=10**8)
     parts = [lax.ppermute(dpart, "tm", y_shift(d)) for d in range(1, NY)]
     grad = final(*inputs, collected)

time: 115 us -> 112 us (0.974)
  waiting for transfers between devices: 34.8 us -> 45.3 us
  starting transfers between devices: 55.7 us -> 45.9 us
  local copies, waits for them, and re-layouts: 9.03 us -> 5.12 us
    ppermute x7 -> x0, starting transfers between devices: 16.9 us -> none  [work(): moved = [lax.ppermute(both[d], 'blk', z_shift(d)) for d in range(1, NZ)]]
    all_to_all x1 -> x2, waiting for transfers between devices: 0.01 us -> 12 us  [exchange(): lax.all_to_all(value, 'blk', 0, 0, axis_index_groups=groups, tiled=True)]
    all_to_all x1 -> x2, starting transfers between devices: 7.79 us -> 13.7 us  [exchange(): lax.all_to_all(value, 'blk', 0, 0, axis_index_groups=groups, tiled=True)]
    unnamed x34 -> x26, local copies, waits for them, and re-layouts: 7.67 us -> 3.76 us
    ppermute x7 -> x0, waiting for transfers between devices: 2.45 us -> none  [work(): moved = [lax.ppermute(both[d], 'blk', z_shift(d)) for d in range(1, NZ)]]
  transfers between devices with their start and end apart: 31 -> 25, of which waited for: 13 -> 12; matrix products, arithmetic and copies ran while one was open for 1% -> 1% of each run, Pallas kernels for 11% -> 12%
where the time goes in v1:
time: 112 us
  starting transfers between devices  45.9 us (41%)
  waiting for transfers between devices  45.3 us (40%)
  Pallas kernels  14.5 us (13%)
  local copies, waits for them, and re-layouts  5.12 us (5%)
    ppermute x6, waiting for transfers between devices, work(): moved = [lax.ppermute(both[d], 'blk', x_shift(d)) for d in range(1, NX)]  23.3 us
    all_to_all x2, starting transfers between devices, exchange(): lax.all_to_all(value, 'blk', 0, 0, axis_index_groups=groups, tiled=True)  13.7 us
    all_to_all x2, waiting for transfers between devices, exchange(): lax.all_to_all(value, 'blk', 0, 0, axis_index_groups=groups, tiled=True)  12 us
    pallas_call x11, Pallas kernels, call(): pl.pallas_call(body, out_shape=out_shape, in_specs=[pl.BlockSpec(memory_s...  11.1 us
    ppermute x6, starting transfers between devices, work(): moved = [lax.ppermute(both[d], 'blk', x_shift(d)) for d in range(1, NX)]  10.4 us
    ppermute x2, starting transfers between devices, work(): far_b = lax.ppermute(high_b, 'tm', down)  5.42 us
    ppermute x2, starting transfers between devices, work(): high_b = lax.ppermute(mine[1], 'tm', down)  4.98 us
    unnamed x26, local copies, waits for them, and re-layouts  3.76 us
  transfers between devices with their start and end apart: 25, of which 12 were waited for; matrix products, arithmetic and copies ran while one was open for 1% of the time, Pallas kernels for 12%

profile of v1, /device:TPU:2, one launch (start us, length us, event | category | flops | bytes accessed | tf_op | source)
XLA Modules:
  0.0 111.7 jit_solution(16530746270882432549)
XLA Ops:
  2.0 1.7 %collective-permute-start.10 = (bf16[12,64,128]{2,1,0:T(8,128)(2,1)S(1)}, bf16[12,64,128]{2,1,0:T(8,128)(2,1)S(1)}, u32[]{:S(2)}, u32[]{:S(2)}) collective-permute-start(bf16[12,64,128]{2,1,0:T(8,128)(2,1)S(1)} %get-tuple-element.33.refs_0_), channel_id=1, source_target_pairs={{0,64},{64,128},{128,192},{192,0},{1,65},{65,129},{129,193},{193,1... | collective-permute-start | bytes 589832 | tf_op jit(solution)/shard_map/ppermute | solution.py:233
  3.7 1.7 %collective-permute-start.14 = (bf16[12,64,128]{2,1,0:T(8,128)(2,1)S(1)}, bf16[12,64,128]{2,1,0:T(8,128)(2,1)}, u32[]{:S(2)}, u32[]{:S(2)}) collective-permute-start(bf16[12,64,128]{2,1,0:T(8,128)(2,1)S(1)} %get-tuple-element.30.refs_4_), channel_id=1, source_target_pairs={{0,192},{64,0},{128,64},{192,128},{1,193},{65,1},{129,65},{193,129... | collective-permute-start | bytes 589832 | tf_op jit(solution)/shard_map/ppermute | solution.py:234
  5.3 1.8 %collective-permute-start.11 = (bf16[12,64,128]{2,1,0:T(8,128)(2,1)S(1)}, bf16[12,64,128]{2,1,0:T(8,128)(2,1)}, u32[]{:S(2)}, u32[]{:S(2)}) collective-permute-start(bf16[12,64,128]{2,1,0:T(8,128)(2,1)S(1)} %get-tuple-element.33.refs_0_), channel_id=1, source_target_pairs={{0,192},{64,0},{128,64},{192,128},{1,193},{65,1},{129,65},{193,129... | collective-permute-start | bytes 589832 | tf_op jit(solution)/shard_map/ppermute | solution.py:236
  7.4 2.7 %collective-permute-done.10.refs_1_ = bf16[12,64,128]{2,1,0:T(8,128)(2,1)S(1)} collective-permute-done((bf16[12,64,128]{2,1,0:T(8,128)(2,1)S(1)}, bf16[12,64,128]{2,1,0:T(8,128)(2,1)S(1)}, u32[]{:S(2)}, u32[]{:S(2)}) %collective-permute-start.10) | collective-permute-done | bytes 196640 | tf_op jit(solution)/shard_map/ppermute | solution.py:233
  10.1 1.4 %collective-permute-start.12 = (bf16[12,64,128]{2,1,0:T(8,128)(2,1)S(1)}, bf16[12,64,128]{2,1,0:T(8,128)(2,1)}, u32[]{:S(2)}, u32[]{:S(2)}) collective-permute-start(bf16[12,64,128]{2,1,0:T(8,128)(2,1)S(1)} %collective-permute-done.10.refs_1_), channel_id=1, source_target_pairs={{0,64},{64,128},{128,192},{192,0},{1,65},{65,129},{129,193},{193,1... | collective-permute-start | bytes 589832 | tf_op jit(solution)/shard_map/ppermute | solution.py:237
  11.6 2.9 %collective-permute-start.15 = (bf16[12,64,128]{2,1,0:T(8,128)(2,1)}, bf16[12,64,128]{2,1,0:T(8,128)(2,1)}, u32[]{:S(2)}, u32[]{:S(2)}) collective-permute-start(bf16[12,64,128]{2,1,0:T(8,128)(2,1)} %collective-permute-done.14.refs_6_), channel_id=1, source_target_pairs={{0,192},{64,0},{128,64},{192,128},{1,193},{65,1},{129,65},{193,129... | collective-permute-start | bytes 589832 | tf_op jit(solution)/shard_map/ppermute | solution.py:238
  15.7 1.8 %shard_map.77 = (bf16[2,128,128]{2,1,0:T(8,128)(2,1)S(1)}, bf16[2,2,128,256]{3,2,1,0:T(8,128)(2,1)S(1)}) custom-call(bf16[128,4096]{1,0:T(8,128)(2,1)S(1)} %bitcast.14, bf16[128,4096]{1,0:T(8,128)(2,1)S(1)} %bitcast.17, f32[2,4096]{1,0:T(2,128)S(1)} %bitcast.20), custom_call_target="tpu_custom_call" | custom-call | flops 1000000000 | bytes 2129920 | tf_op jit(solution)/shard_map/pallas_call | solution.py:41
  17.5 3.3 %collective-permute-start.4 = (bf16[12,64,128]{2,1,0:T(8,128)(2,1)S(1)}, bf16[12,64,128]{2,1,0:T(8,128)(2,1)S(1)}, u32[]{:S(2)}, u32[]{:S(2)}) collective-permute-start(bf16[12,64,128]{2,1,0:T(8,128)(2,1)S(1)} %get-tuple-element.31.refs_4_), channel_id=1, source_target_pairs={{0,192},{64,0},{128,64},{192,128},{1,193},{65,1},{129,65},{193,129... | collective-permute-start | bytes 589832 | tf_op jit(solution)/shard_map/ppermute | solution.py:234
  20.9 2.3 %shard_map.82 = (bf16[33,2,64,128]{3,2,1,0:T(8,128)(2,1)S(1)}, bf16[33,2,64,128]{3,2,1,0:T(8,128)(2,1)S(1)}) custom-call(s32[1,24]{1,0:T(1,128)S(1)} %copy-done.4, s32[8,4]{1,0:T(8,128)S(1)} %copy.8.cos_ref, bf16[2,128,128]{2,1,0:T(8,128)(2,1)S(1)} %get-tuple-element.16.metric_ref, bf16[12,64,128]{2,1,0:T(8,128)(2,1)S(1)} %get-tuple-element.33.refs_0_, ...), custom_call_target="tpu_custom_call" | custom-call | flops 1000000000 | bytes 1638624 | tf_op jit(solution)/shard_map/pallas_call | solution.py:41
  26.8 2.6 %collective-permute-start.5 = (bf16[12,64,128]{2,1,0:T(8,128)(2,1)S(1)}, bf16[12,64,128]{2,1,0:T(8,128)(2,1)S(1)}, u32[]{:S(2)}, u32[]{:S(2)}) collective-permute-start(bf16[12,64,128]{2,1,0:T(8,128)(2,1)S(1)} %collective-permute-done.4.refs_6_), channel_id=1, source_target_pairs={{0,192},{64,0},{128,64},{192,128},{1,193},{65,1},{129,65},{193,129... | collective-permute-start | bytes 589832 | tf_op jit(solution)/shard_map/ppermute | solution.py:238
  29.3 1.8 %collective-permute-done.1.refs_2_ = bf16[12,64,128]{2,1,0:T(8,128)(2,1)S(1)} collective-permute-done((bf16[12,64,128]{2,1,0:T(8,128)(2,1)S(1)}, bf16[12,64,128]{2,1,0:T(8,128)(2,1)S(1)}, u32[]{:S(2)}, u32[]{:S(2)}) %collective-permute-start.1) | collective-permute-done | bytes 196640 | tf_op jit(solution)/shard_map/ppermute | solution.py:236
  31.2 2.0 %collective-permute-done.3.refs_5_ = bf16[12,64,128]{2,1,0:T(8,128)(2,1)S(1)} collective-permute-done((bf16[12,64,128]{2,1,0:T(8,128)(2,1)S(1)}, bf16[12,64,128]{2,1,0:T(8,128)(2,1)S(1)}, u32[]{:S(2)}, u32[]{:S(2)}) %collective-permute-start.3) | collective-permute-done | bytes 196640 | tf_op jit(solution)/shard_map/ppermute | solution.py:235
  33.1 3.4 %collective-permute-done.2.refs_3_ = bf16[12,64,128]{2,1,0:T(8,128)(2,1)S(1)} collective-permute-done((bf16[12,64,128]{2,1,0:T(8,128)(2,1)S(1)}, bf16[12,64,128]{2,1,0:T(8,128)(2,1)S(1)}, u32[]{:S(2)}, u32[]{:S(2)}) %collective-permute-start.2) | collective-permute-done | bytes 196640 | tf_op jit(solution)/shard_map/ppermute | solution.py:237
  38.4 2.6 %shard_map.78 = (bf16[33,2,64,128]{3,2,1,0:T(8,128)(2,1)}, bf16[33,2,64,128]{3,2,1,0:T(8,128)(2,1)S(1)}) custom-call(s32[1,24]{1,0:T(1,128)S(1)} %copy-done.4, s32[8,4]{1,0:T(8,128)S(1)} %copy.8.cos_ref, bf16[2,128,128]{2,1,0:T(8,128)(2,1)S(1)} %get-tuple-element.16.metric_ref, bf16[12,64,128]{2,1,0:T(8,128)(2,1)S(1)} %copy-done.1, ...), custom_call_target="tpu_custom_call" | custom-call | flops 1000000000 | bytes 1638624 | tf_op jit(solution)/shard_map/pallas_call | solution.py:41
  41.2 1.6 %collective-permute-start.17 = (bf16[8,2,64,128]{3,2,1,0:T(8,128)(2,1)S(1)}, bf16[8,2,64,128]{3,2,1,0:T(8,128)(2,1)S(1)}, u32[]{:S(2)}, u32[]{:S(2)}) collective-permute-start(bf16[8,2,64,128]{3,2,1,0:T(8,128)(2,1)S(1)} %get-tuple-element.26), channel_id=1, source_target_pairs={{0,16},{1,17},{2,18},{3,19},{4,20},{5,21},{6,22},{7,23},{8,24},{9,... | collective-permute-start | bytes 786440 | tf_op jit(solution)/shard_map/ppermute | solution.py:254
  42.8 4.3 %collective-permute-start.18 = (bf16[8,2,64,128]{3,2,1,0:T(8,128)(2,1)S(1)}, bf16[8,2,64,128]{3,2,1,0:T(8,128)(2,1)S(1)}, u32[]{:S(2)}, u32[]{:S(2)}) collective-permute-start(bf16[8,2,64,128]{3,2,1,0:T(8,128)(2,1)S(1)} %get-tuple-element.27), channel_id=1, source_target_pairs={{0,32},{1,33},{2,34},{3,35},{4,36},{5,37},{6,38},{7,39},{8,40},{9,... | collective-permute-start | bytes 786440 | tf_op jit(solution)/shard_map/ppermute | solution.py:254
  47.1 5.1 %collective-permute-done.17.b_ref = bf16[8,2,64,128]{3,2,1,0:T(8,128)(2,1)S(1)} collective-permute-done((bf16[8,2,64,128]{3,2,1,0:T(8,128)(2,1)S(1)}, bf16[8,2,64,128]{3,2,1,0:T(8,128)(2,1)S(1)}, u32[]{:S(2)}, u32[]{:S(2)}) %collective-permute-start.17) | collective-permute-done | bytes 262176 | tf_op jit(solution)/shard_map/ppermute | solution.py:254
  52.2 2.1 %collective-permute-done.18.c_ref = bf16[8,2,64,128]{3,2,1,0:T(8,128)(2,1)S(1)} collective-permute-done((bf16[8,2,64,128]{3,2,1,0:T(8,128)(2,1)S(1)}, bf16[8,2,64,128]{3,2,1,0:T(8,128)(2,1)S(1)}, u32[]{:S(2)}, u32[]{:S(2)}) %collective-permute-start.18) | collective-permute-done | bytes 262176 | tf_op jit(solution)/shard_map/ppermute | solution.py:254
  54.3 5.1 %collective-permute-done.19.d_ref = bf16[8,2,64,128]{3,2,1,0:T(8,128)(2,1)S(1)} collective-permute-done((bf16[8,2,64,128]{3,2,1,0:T(8,128)(2,1)S(1)}, bf16[8,2,64,128]{3,2,1,0:T(8,128)(2,1)S(1)}, u32[]{:S(2)}, u32[]{:S(2)}) %collective-permute-start.19) | collective-permute-done | bytes 262176 | tf_op jit(solution)/shard_map/ppermute | solution.py:254
  60.3 6.7 %all-to-all-start.1 = ((bf16[8,2,64,128]{3,2,1,0:T(8,128)(2,1)}), bf16[8,2,64,128]{3,2,1,0:T(8,128)(2,1)S(1)}, u32[]{:S(2)}, u32[]{:S(2)}) async-start(bf16[8,2,64,128]{3,2,1,0:T(8,128)(2,1)} %shard_map.84), calls=%async_computation.1 | async-start | bytes 524288 | tf_op jit(solution)/shard_map/all_to_all | solution.py:218
  67.0 1.5 %shard_map.79 = (bf16[8,2,64,128]{3,2,1,0:T(8,128)(2,1)S(1)}, bf16[8,2,64,128]{3,2,1,0:T(8,128)(2,1)S(1)}, bf16[8,2,64,128]{3,2,1,0:T(8,128)(2,1)S(1)}, bf16[8,2,64,128]{3,2,1,0:T(8,128)(2,1)S(1)}) custom-call(bf16[33,2,64,128]{3,2,1,0:T(8,128)(2,1)S(1)} %get-tuple-element.17.a_ref, bf16[33,2,64,128]{3,2,1,0:T(8,128)(2,1)} %collective-permute-done.6.b_ref), custom_call_target="tpu_custom_call" | custom-call | flops 10000000 | bytes 2162688 | tf_op jit(solution)/shard_map/pallas_call | solution.py:41
  68.5 1.4 %collective-permute-start.7 = (bf16[8,2,64,128]{3,2,1,0:T(8,128)(2,1)S(1)}, bf16[8,2,64,128]{3,2,1,0:T(8,128)(2,1)S(1)}, u32[]{:S(2)}, u32[]{:S(2)}) collective-permute-start(bf16[8,2,64,128]{3,2,1,0:T(8,128)(2,1)S(1)} %get-tuple-element.20), channel_id=1, source_target_pairs={{0,16},{1,17},{2,18},{3,19},{4,20},{5,21},{6,22},{7,23},{8,24},{9,... | collective-permute-start | bytes 786440 | tf_op jit(solution)/shard_map/ppermute | solution.py:254
  69.9 1.5 %collective-permute-start.8 = (bf16[8,2,64,128]{3,2,1,0:T(8,128)(2,1)S(1)}, bf16[8,2,64,128]{3,2,1,0:T(8,128)(2,1)S(1)}, u32[]{:S(2)}, u32[]{:S(2)}) collective-permute-start(bf16[8,2,64,128]{3,2,1,0:T(8,128)(2,1)S(1)} %get-tuple-element.21), channel_id=1, source_target_pairs={{0,32},{1,33},{2,34},{3,35},{4,36},{5,37},{6,38},{7,39},{8,40},{9,... | collective-permute-start | bytes 786440 | tf_op jit(solution)/shard_map/ppermute | solution.py:254
  71.4 1.7 %collective-permute-start.9 = (bf16[8,2,64,128]{3,2,1,0:T(8,128)(2,1)S(1)}, bf16[8,2,64,128]{3,2,1,0:T(8,128)(2,1)S(1)}, u32[]{:S(2)}, u32[]{:S(2)}) collective-permute-start(bf16[8,2,64,128]{3,2,1,0:T(8,128)(2,1)S(1)} %get-tuple-element.22), channel_id=1, source_target_pairs={{0,48},{1,49},{2,50},{3,51},{4,52},{5,53},{6,54},{7,55},{8,56},{9,... | collective-permute-start | bytes 786440 | tf_op jit(solution)/shard_map/ppermute | solution.py:254
  73.0 4.8 %collective-permute-done.7.b_ref = bf16[8,2,64,128]{3,2,1,0:T(8,128)(2,1)S(1)} collective-permute-done((bf16[8,2,64,128]{3,2,1,0:T(8,128)(2,1)S(1)}, bf16[8,2,64,128]{3,2,1,0:T(8,128)(2,1)S(1)}, u32[]{:S(2)}, u32[]{:S(2)}) %collective-permute-start.7) | collective-permute-done | bytes 262176 | tf_op jit(solution)/shard_map/ppermute | solution.py:254
  77.8 2.8 %collective-permute-done.8.c_ref = bf16[8,2,64,128]{3,2,1,0:T(8,128)(2,1)S(1)} collective-permute-done((bf16[8,2,64,128]{3,2,1,0:T(8,128)(2,1)S(1)}, bf16[8,2,64,128]{3,2,1,0:T(8,128)(2,1)S(1)}, u32[]{:S(2)}, u32[]{:S(2)}) %collective-permute-start.8) | collective-permute-done | bytes 262176 | tf_op jit(solution)/shard_map/ppermute | solution.py:254
  80.6 3.4 %collective-permute-done.9.d_ref = bf16[8,2,64,128]{3,2,1,0:T(8,128)(2,1)S(1)} collective-permute-done((bf16[8,2,64,128]{3,2,1,0:T(8,128)(2,1)S(1)}, bf16[8,2,64,128]{3,2,1,0:T(8,128)(2,1)S(1)}, u32[]{:S(2)}, u32[]{:S(2)}) %collective-permute-start.9) | collective-permute-done | bytes 262176 | tf_op jit(solution)/shard_map/ppermute | solution.py:254
  84.9 6.9 %all-to-all-start = ((bf16[8,2,64,128]{3,2,1,0:T(8,128)(2,1)}), bf16[8,2,64,128]{3,2,1,0:T(8,128)(2,1)S(1)}, u32[]{:S(2)}, u32[]{:S(2)}) async-start(bf16[8,2,64,128]{3,2,1,0:T(8,128)(2,1)} %shard_map.80), calls=%async_computation | async-start | bytes 524288 | tf_op jit(solution)/shard_map/all_to_all | solution.py:218
  91.8 12.0 %all-to-all-done.in_ref = bf16[8,2,64,128]{3,2,1,0:T(8,128)(2,1)S(1)} async-done(((bf16[8,2,64,128]{3,2,1,0:T(8,128)(2,1)}), bf16[8,2,64,128]{3,2,1,0:T(8,128)(2,1)S(1)}, u32[]{:S(2)}, u32[]{:S(2)}) %all-to-all-start) | async-done | bytes 262176 | tf_op jit(solution)/shard_map/all_to_all | solution.py:218
  104.2 1.8 %collective-permute-start.21 = (bf16[128,128]{1,0:T(8,128)(2,1)S(1)}, bf16[128,128]{1,0:T(8,128)(2,1)S(1)}, u32[]{:S(2)}, u32[]{:S(2)}) collective-permute-start(bf16[128,128]{1,0:T(8,128)(2,1)S(1)} %shard_map.86.a_ref), channel_id=1, source_target_pairs={{0,128},{64,192},{128,0},{192,64},{1,129},{65,193},{129,1},{193,65... | collective-permute-start | bytes 98312 | tf_op jit(solution)/shard_map/ppermute | solution.py:259
  106.1 1.5 %collective-permute-start.22 = (bf16[128,128]{1,0:T(8,128)(2,1)S(1)}, bf16[128,128]{1,0:T(8,128)(2,1)S(1)}, u32[]{:S(2)}, u32[]{:S(2)}) collective-permute-start(bf16[128,128]{1,0:T(8,128)(2,1)S(1)} %shard_map.86.a_ref), channel_id=1, source_target_pairs={{0,192},{64,0},{128,64},{192,128},{1,193},{65,1},{129,65},{193,129... | collective-permute-start | bytes 98312 | tf_op jit(solution)/shard_map/ppermute | solution.py:259
  107.6 3.4 %final.1 = bf16[2,128,2,2048]{3,2,1,0:T(2,128)(2,1)} custom-call(bf16[128,4096]{1,0:T(8,128)(2,1)S(1)} %bitcast.15, bf16[128,4096]{1,0:T(8,128)(2,1)S(1)} %bitcast.16, bf16[128,4096]{1,0:T(8,128)(2,1)S(1)} %bitcast.18, bf16[128,4096]{1,0:T(8,128)(2,1)S(1)} %bitcast.19, f32[2,4096]{1,0:T(2,128)S(1)} %bitcast.21, f32[2,4096]{1,0:T(2,128)S(1)} %bitcast.22, ...), custom_call_target="tpu_custom_call" | custom-call | flops 1000000000 | bytes 4194304 | tf_op jit(solution)/shard_map/final/pallas_call | solution.py:185
  (57 shorter events, 11.4 us)
Async XLA Ops:
  0.6 13.8 %copy-start.7 = (bf16[128,2,2048]{2,1,0:T(2,128)(2,1)S(1)}, bf16[128,2,2048]{2,1,0:T(2,128)(2,1)}, u32[]{:S(2)}) copy-start(bf16[128,2,2048]{2,1,0:T(2,128)(2,1)} %param.9) | copy-start | bytes 3145732
  2.0 21.3 %copy-start = (bf16[12,64,128]{2,1,0:T(8,128)(2,1)}, bf16[12,64,128]{2,1,0:T(8,128)(2,1)S(1)}, u32[]{:S(2)}) copy-start(bf16[12,64,128]{2,1,0:T(8,128)(2,1)S(1)} %get-tuple-element.32.refs_0_) | copy-start | bytes 589828
  2.0 12.8 %copy-start.8 = (bf16[128,2,2048]{2,1,0:T(2,128)(2,1)S(1)}, bf16[128,2,2048]{2,1,0:T(2,128)(2,1)}, u32[]{:S(2)}) copy-start(bf16[128,2,2048]{2,1,0:T(2,128)(2,1)} %param.10) | copy-start | bytes 3145732
  2.0 8.1 %collective-permute-start.10 = (bf16[12,64,128]{2,1,0:T(8,128)(2,1)S(1)}, bf16[12,64,128]{2,1,0:T(8,128)(2,1)S(1)}, u32[]{:S(2)}, u32[]{:S(2)}) collective-permute-start(bf16[12,64,128]{2,1,0:T(8,128)(2,1)S(1)} %get-tuple-element.33.refs_0_), channel_id=1, source_target_pairs={{0,64},{64,128},{128,192},{192,0},{1,65},{65,129},{129,193},{193,1... | collective-permute-start | bytes 589832 | tf_op jit(solution)/shard_map/ppermute | solution.py:233
  3.7 7.9 %collective-permute-start.14 = (bf16[12,64,128]{2,1,0:T(8,128)(2,1)S(1)}, bf16[12,64,128]{2,1,0:T(8,128)(2,1)}, u32[]{:S(2)}, u32[]{:S(2)}) collective-permute-start(bf16[12,64,128]{2,1,0:T(8,128)(2,1)S(1)} %get-tuple-element.30.refs_4_), channel_id=1, source_target_pairs={{0,192},{64,0},{128,64},{192,128},{1,193},{65,1},{129,65},{193,129... | collective-permute-start | bytes 589832 | tf_op jit(solution)/shard_map/ppermute | solution.py:234
  5.3 12.2 %collective-permute-start.11 = (bf16[12,64,128]{2,1,0:T(8,128)(2,1)S(1)}, bf16[12,64,128]{2,1,0:T(8,128)(2,1)}, u32[]{:S(2)}, u32[]{:S(2)}) collective-permute-start(bf16[12,64,128]{2,1,0:T(8,128)(2,1)S(1)} %get-tuple-element.33.refs_0_), channel_id=1, source_target_pairs={{0,192},{64,0},{128,64},{192,128},{1,193},{65,1},{129,65},{193,129... | collective-permute-start | bytes 589832 | tf_op jit(solution)/shard_map/ppermute | solution.py:236
  7.1 13.7 %collective-permute-start.13 = (bf16[12,64,128]{2,1,0:T(8,128)(2,1)S(1)}, bf16[12,64,128]{2,1,0:T(8,128)(2,1)}, u32[]{:S(2)}, u32[]{:S(2)}) collective-permute-start(bf16[12,64,128]{2,1,0:T(8,128)(2,1)S(1)} %get-tuple-element.30.refs_4_), channel_id=1, source_target_pairs={{0,64},{64,128},{128,192},{192,0},{1,65},{65,129},{129,193},{193,1... | collective-permute-start | bytes 589832 | tf_op jit(solution)/shard_map/ppermute | solution.py:235
  10.1 10.8 %collective-permute-start.12 = (bf16[12,64,128]{2,1,0:T(8,128)(2,1)S(1)}, bf16[12,64,128]{2,1,0:T(8,128)(2,1)}, u32[]{:S(2)}, u32[]{:S(2)}) collective-permute-start(bf16[12,64,128]{2,1,0:T(8,128)(2,1)S(1)} %collective-permute-done.10.refs_1_), channel_id=1, source_target_pairs={{0,64},{64,128},{128,192},{192,0},{1,65},{65,129},{129,193},{193,1... | collective-permute-start | bytes 589832 | tf_op jit(solution)/shard_map/ppermute | solution.py:237
  11.6 9.3 %collective-permute-start.15 = (bf16[12,64,128]{2,1,0:T(8,128)(2,1)}, bf16[12,64,128]{2,1,0:T(8,128)(2,1)}, u32[]{:S(2)}, u32[]{:S(2)}) collective-permute-start(bf16[12,64,128]{2,1,0:T(8,128)(2,1)} %collective-permute-done.14.refs_6_), channel_id=1, source_target_pairs={{0,192},{64,0},{128,64},{192,128},{1,193},{65,1},{129,65},{193,129... | collective-permute-start | bytes 589832 | tf_op jit(solution)/shard_map/ppermute | solution.py:238
  14.4 11.0 %collective-permute-start = (bf16[12,64,128]{2,1,0:T(8,128)(2,1)S(1)}, bf16[12,64,128]{2,1,0:T(8,128)(2,1)S(1)}, u32[]{:S(2)}, u32[]{:S(2)}) collective-permute-start(bf16[12,64,128]{2,1,0:T(8,128)(2,1)S(1)} %get-tuple-element.32.refs_0_), channel_id=1, source_target_pairs={{0,64},{64,128},{128,192},{192,0},{1,65},{65,129},{129,193},{193,1... | collective-permute-start | bytes 589832 | tf_op jit(solution)/shard_map/ppermute | solution.py:233
  15.7 5.2 %copy-start.4 = (s32[1,24]{1,0:T(1,128)S(1)}, s32[1,24]{1,0:T(1,128)}, u32[]{:S(2)}) copy-start(s32[1,24]{1,0:T(1,128)} %part_ref.3) | copy-start | bytes 292
  17.5 5.7 %copy-start.5 = (bf16[2,2,128,256]{3,2,1,0:T(8,128)(2,1)}, bf16[2,2,128,256]{3,2,1,0:T(8,128)(2,1)S(1)}, u32[]{:S(2)}) copy-start(bf16[2,2,128,256]{3,2,1,0:T(8,128)(2,1)S(1)} %get-tuple-element.29.gram_ref) | copy-start | bytes 786436
  17.5 9.2 %collective-permute-start.4 = (bf16[12,64,128]{2,1,0:T(8,128)(2,1)S(1)}, bf16[12,64,128]{2,1,0:T(8,128)(2,1)S(1)}, u32[]{:S(2)}, u32[]{:S(2)}) collective-permute-start(bf16[12,64,128]{2,1,0:T(8,128)(2,1)S(1)} %get-tuple-element.31.refs_4_), channel_id=1, source_target_pairs={{0,192},{64,0},{128,64},{192,128},{1,193},{65,1},{129,65},{193,129... | collective-permute-start | bytes 589832 | tf_op jit(solution)/shard_map/ppermute | solution.py:234
  23.2 17.7 %collective-permute-start.16 = (bf16[33,2,64,128]{3,2,1,0:T(8,128)(2,1)S(1)}, bf16[33,2,64,128]{3,2,1,0:T(8,128)(2,1)S(1)}, u32[]{:S(2)}, u32[]{:S(2)}) collective-permute-start(bf16[33,2,64,128]{3,2,1,0:T(8,128)(2,1)S(1)} %get-tuple-element.24), channel_id=1, source_target_pairs={{0,1},{1,0},{2,3},{3,2},{4,5},{5,4},{6,7},{7,6},{8,9},{9,8},{10,11... | collective-permute-start | bytes 3244040 | tf_op jit(solution)/shard_map/ppermute | solution.py:252
  23.3 7.8 %collective-permute-start.1 = (bf16[12,64,128]{2,1,0:T(8,128)(2,1)S(1)}, bf16[12,64,128]{2,1,0:T(8,128)(2,1)S(1)}, u32[]{:S(2)}, u32[]{:S(2)}) collective-permute-start(bf16[12,64,128]{2,1,0:T(8,128)(2,1)S(1)} %get-tuple-element.32.refs_0_), channel_id=1, source_target_pairs={{0,192},{64,0},{128,64},{192,128},{1,193},{65,1},{129,65},{193,129... | collective-permute-start | bytes 589832 | tf_op jit(solution)/shard_map/ppermute | solution.py:236
  24.1 9.0 %collective-permute-start.3 = (bf16[12,64,128]{2,1,0:T(8,128)(2,1)S(1)}, bf16[12,64,128]{2,1,0:T(8,128)(2,1)S(1)}, u32[]{:S(2)}, u32[]{:S(2)}) collective-permute-start(bf16[12,64,128]{2,1,0:T(8,128)(2,1)S(1)} %get-tuple-element.31.refs_4_), channel_id=1, source_target_pairs={{0,64},{64,128},{128,192},{192,0},{1,65},{65,129},{129,193},{193,1... | collective-permute-start | bytes 589832 | tf_op jit(solution)/shard_map/ppermute | solution.py:235
  25.4 11.1 %collective-permute-start.2 = (bf16[12,64,128]{2,1,0:T(8,128)(2,1)S(1)}, bf16[12,64,128]{2,1,0:T(8,128)(2,1)S(1)}, u32[]{:S(2)}, u32[]{:S(2)}) collective-permute-start(bf16[12,64,128]{2,1,0:T(8,128)(2,1)S(1)} %collective-permute-done.refs_1_), channel_id=1, source_target_pairs={{0,64},{64,128},{128,192},{192,0},{1,65},{65,129},{129,193},{193,1... | collective-permute-start | bytes 589832 | tf_op jit(solution)/shard_map/ppermute | solution.py:237
  26.8 9.7 %collective-permute-start.5 = (bf16[12,64,128]{2,1,0:T(8,128)(2,1)S(1)}, bf16[12,64,128]{2,1,0:T(8,128)(2,1)S(1)}, u32[]{:S(2)}, u32[]{:S(2)}) collective-permute-start(bf16[12,64,128]{2,1,0:T(8,128)(2,1)S(1)} %collective-permute-done.4.refs_6_), channel_id=1, source_target_pairs={{0,192},{64,0},{128,64},{192,128},{1,193},{65,1},{129,65},{193,129... | collective-permute-start | bytes 589832 | tf_op jit(solution)/shard_map/ppermute | solution.py:238
  36.5 0.9 copy-start.1
  40.9 26.1 %collective-permute-start.6 = (bf16[33,2,64,128]{3,2,1,0:T(8,128)(2,1)}, bf16[33,2,64,128]{3,2,1,0:T(8,128)(2,1)}, u32[]{:S(2)}, u32[]{:S(2)}) collective-permute-start(bf16[33,2,64,128]{3,2,1,0:T(8,128)(2,1)} %get-tuple-element.18), channel_id=1, source_target_pairs={{0,1},{1,0},{2,3},{3,2},{4,5},{5,4},{6,7},{7,6},{8,9},{9,8},{10,11... | collective-permute-start | bytes 3244040 | tf_op jit(solution)/shard_map/ppermute | solution.py:252
  41.2 11.0 %collective-permute-start.17 = (bf16[8,2,64,128]{3,2,1,0:T(8,128)(2,1)S(1)}, bf16[8,2,64,128]{3,2,1,0:T(8,128)(2,1)S(1)}, u32[]{:S(2)}, u32[]{:S(2)}) collective-permute-start(bf16[8,2,64,128]{3,2,1,0:T(8,128)(2,1)S(1)} %get-tuple-element.26), channel_id=1, source_target_pairs={{0,16},{1,17},{2,18},{3,19},{4,20},{5,21},{6,22},{7,23},{8,24},{9,... | collective-permute-start | bytes 786440 | tf_op jit(solution)/shard_map/ppermute | solution.py:254
  42.8 11.5 %collective-permute-start.18 = (bf16[8,2,64,128]{3,2,1,0:T(8,128)(2,1)S(1)}, bf16[8,2,64,128]{3,2,1,0:T(8,128)(2,1)S(1)}, u32[]{:S(2)}, u32[]{:S(2)}) collective-permute-start(bf16[8,2,64,128]{3,2,1,0:T(8,128)(2,1)S(1)} %get-tuple-element.27), channel_id=1, source_target_pairs={{0,32},{1,33},{2,34},{3,35},{4,36},{5,37},{6,38},{7,39},{8,40},{9,... | collective-permute-start | bytes 786440 | tf_op jit(solution)/shard_map/ppermute | solution.py:254
  47.1 12.3 %collective-permute-start.19 = (bf16[8,2,64,128]{3,2,1,0:T(8,128)(2,1)S(1)}, bf16[8,2,64,128]{3,2,1,0:T(8,128)(2,1)S(1)}, u32[]{:S(2)}, u32[]{:S(2)}) collective-permute-start(bf16[8,2,64,128]{3,2,1,0:T(8,128)(2,1)S(1)} %get-tuple-element.28), channel_id=1, source_target_pairs={{0,48},{1,49},{2,50},{3,51},{4,52},{5,53},{6,54},{7,55},{8,56},{9,... | collective-permute-start | bytes 786440 | tf_op jit(solution)/shard_map/ppermute | solution.py:254
  60.3 24.6 %all-to-all-start.1 = ((bf16[8,2,64,128]{3,2,1,0:T(8,128)(2,1)}), bf16[8,2,64,128]{3,2,1,0:T(8,128)(2,1)S(1)}, u32[]{:S(2)}, u32[]{:S(2)}) async-start(bf16[8,2,64,128]{3,2,1,0:T(8,128)(2,1)} %shard_map.84), calls=%async_computation.1 | async-start | bytes 524288 | tf_op jit(solution)/shard_map/all_to_all | solution.py:218
  68.5 9.3 %collective-permute-start.7 = (bf16[8,2,64,128]{3,2,1,0:T(8,128)(2,1)S(1)}, bf16[8,2,64,128]{3,2,1,0:T(8,128)(2,1)S(1)}, u32[]{:S(2)}, u32[]{:S(2)}) collective-permute-start(bf16[8,2,64,128]{3,2,1,0:T(8,128)(2,1)S(1)} %get-tuple-element.20), channel_id=1, source_target_pairs={{0,16},{1,17},{2,18},{3,19},{4,20},{5,21},{6,22},{7,23},{8,24},{9,... | collective-permute-start | bytes 786440 | tf_op jit(solution)/shard_map/ppermute | solution.py:254
  69.9 10.7 %collective-permute-start.8 = (bf16[8,2,64,128]{3,2,1,0:T(8,128)(2,1)S(1)}, bf16[8,2,64,128]{3,2,1,0:T(8,128)(2,1)S(1)}, u32[]{:S(2)}, u32[]{:S(2)}) collective-permute-start(bf16[8,2,64,128]{3,2,1,0:T(8,128)(2,1)S(1)} %get-tuple-element.21), channel_id=1, source_target_pairs={{0,32},{1,33},{2,34},{3,35},{4,36},{5,37},{6,38},{7,39},{8,40},{9,... | collective-permute-start | bytes 786440 | tf_op jit(solution)/shard_map/ppermute | solution.py:254
  71.4 12.6 %collective-permute-start.9 = (bf16[8,2,64,128]{3,2,1,0:T(8,128)(2,1)S(1)}, bf16[8,2,64,128]{3,2,1,0:T(8,128)(2,1)S(1)}, u32[]{:S(2)}, u32[]{:S(2)}) collective-permute-start(bf16[8,2,64,128]{3,2,1,0:T(8,128)(2,1)S(1)} %get-tuple-element.22), channel_id=1, source_target_pairs={{0,48},{1,49},{2,50},{3,51},{4,52},{5,53},{6,54},{7,55},{8,56},{9,... | collective-permute-start | bytes 786440 | tf_op jit(solution)/shard_map/ppermute | solution.py:254
  84.0 19.8 %copy-start.6 = (bf16[2,2,128,256]{3,2,1,0:T(8,128)(2,1)S(1)}, bf16[2,2,128,256]{3,2,1,0:T(8,128)(2,1)}, u32[]{:S(2)}) copy-start(bf16[2,2,128,256]{3,2,1,0:T(8,128)(2,1)} %copy-done.5) | copy-start | bytes 786436
  84.9 19.0 %all-to-all-start = ((bf16[8,2,64,128]{3,2,1,0:T(8,128)(2,1)}), bf16[8,2,64,128]{3,2,1,0:T(8,128)(2,1)S(1)}, u32[]{:S(2)}, u32[]{:S(2)}) async-start(bf16[8,2,64,128]{3,2,1,0:T(8,128)(2,1)} %shard_map.80), calls=%async_computation | async-start | bytes 524288 | tf_op jit(solution)/shard_map/all_to_all | solution.py:218
  104.1 6.9 %collective-permute-start.20 = (bf16[128,128]{1,0:T(8,128)(2,1)S(1)}, bf16[128,128]{1,0:T(8,128)(2,1)S(1)}, u32[]{:S(2)}, u32[]{:S(2)}) collective-permute-start(bf16[128,128]{1,0:T(8,128)(2,1)S(1)} %shard_map.86.a_ref), channel_id=1, source_target_pairs={{0,64},{64,128},{128,192},{192,0},{1,65},{65,129},{129,193},{193,1... | collective-permute-start | bytes 98312 | tf_op jit(solution)/shard_map/ppermute | solution.py:259
  104.2 6.8 %collective-permute-start.21 = (bf16[128,128]{1,0:T(8,128)(2,1)S(1)}, bf16[128,128]{1,0:T(8,128)(2,1)S(1)}, u32[]{:S(2)}, u32[]{:S(2)}) collective-permute-start(bf16[128,128]{1,0:T(8,128)(2,1)S(1)} %shard_map.86.a_ref), channel_id=1, source_target_pairs={{0,128},{64,192},{128,0},{192,64},{1,129},{65,193},{129,1},{193,65... | collective-permute-start | bytes 98312 | tf_op jit(solution)/shard_map/ppermute | solution.py:259
  106.1 5.0 %collective-permute-start.22 = (bf16[128,128]{1,0:T(8,128)(2,1)S(1)}, bf16[128,128]{1,0:T(8,128)(2,1)S(1)}, u32[]{:S(2)}, u32[]{:S(2)}) collective-permute-start(bf16[128,128]{1,0:T(8,128)(2,1)S(1)} %shard_map.86.a_ref), channel_id=1, source_target_pairs={{0,192},{64,0},{128,64},{192,128},{1,193},{65,1},{129,65},{193,129... | collective-permute-start | bytes 98312 | tf_op jit(solution)/shard_map/ppermute | solution.py:259
  (4 other events, 3.1 us)

commit v2 on v1

--- a/solution.py
+++ b/solution.py
@@ -177,7 +177,7 @@
 def final(tens, dens, decay, collected):
     block, width = tens.shape
     times = decay.shape[0]
-    half, step = width // 2, 512
+    half, step = width // 2, 1024
     steps = half // step
     views = [pl.BlockSpec((block, step), lambda i, j=j: (0, i + j * steps)) for j in range(2)]
     decays = [pl.BlockSpec((times, step), lambda i, j=j: (0, i + j * steps)) for j in range(2)]
@@ -228,7 +228,9 @@
 
     chis = []
     start = 0
-    for rows in CHUNKS:
+    for c, rows in enumerate(CHUNKS):
+        if c:
+            chi_bar = lax.optimization_barrier((chi_bar, mine))[0]
         mine = [chi_bar[0, 0, h : h + half, start : start + rows, :] for h in (0, half)]
         low_a = lax.ppermute(mine[0], "tm", up)
         high_b = lax.ppermute(mine[1], "tm", down)

time: 112 us -> 112 us (level)
  local copies, waits for them, and re-layouts: 5.12 us -> 6.67 us
  transfers between devices with their start and end apart: 25 -> 25, of which waited for: 12 -> 12; matrix products, arithmetic and copies ran while one was open for 1% -> 2% of each run, Pallas kernels for 12% -> 12%
where the time goes in v2:
time: 112 us
  starting transfers between devices  45.3 us (40%)
  waiting for transfers between devices  44.8 us (40%)
  Pallas kernels  14.1 us (13%)
  local copies, waits for them, and re-layouts  6.67 us (6%)
    ppermute x6, waiting for transfers between devices, work(): moved = [lax.ppermute(both[d], 'blk', x_shift(d)) for d in range(1, NX)]  23.3 us
    all_to_all x2, starting transfers between devices, exchange(): lax.all_to_all(value, 'blk', 0, 0, axis_index_groups=groups, tiled=True)  14.7 us
    all_to_all x2, waiting for transfers between devices, exchange(): lax.all_to_all(value, 'blk', 0, 0, axis_index_groups=groups, tiled=True)  12 us
    pallas_call x11, Pallas kernels, call(): pl.pallas_call(body, out_shape=out_shape, in_specs=[pl.BlockSpec(memory_s...  11.1 us
    ppermute x6, starting transfers between devices, work(): moved = [lax.ppermute(both[d], 'blk', x_shift(d)) for d in range(1, NX)]  9.32 us
    ppermute x2, starting transfers between devices, work(): far_b = lax.ppermute(high_b, 'tm', down)  6.09 us
    unnamed x26, local copies, waits for them, and re-layouts  4.48 us
    ppermute x2, starting transfers between devices, work(): high_b = lax.ppermute(mine[1], 'tm', down)  4.26 us
  transfers between devices with their start and end apart: 25, of which 12 were waited for; matrix products, arithmetic and copies ran while one was open for 2% of the time, Pallas kernels for 12%

profile of v2, /device:TPU:2, one launch (start us, length us, event | category | flops | bytes accessed | tf_op | source)
XLA Modules:
  0.0 111.7 jit_solution(525566827124151663)
XLA Ops:
  1.8 1.7 %collective-permute-start = (bf16[12,64,128]{2,1,0:T(8,128)(2,1)S(1)}, bf16[12,64,128]{2,1,0:T(8,128)(2,1)S(1)}, u32[]{:S(2)}, u32[]{:S(2)}) collective-permute-start(bf16[12,64,128]{2,1,0:T(8,128)(2,1)S(1)} %get-tuple-element.35.refs_0_), channel_id=1, source_target_pairs={{0,64},{64,128},{128,192},{192,0},{1,65},{65,129},{129,193},{193,1... | collective-permute-start | bytes 589832 | tf_op jit(solution)/shard_map/ppermute | solution.py:235
  3.4 1.7 %collective-permute-start.4 = (bf16[12,64,128]{2,1,0:T(8,128)(2,1)S(1)}, bf16[12,64,128]{2,1,0:T(8,128)(2,1)}, u32[]{:S(2)}, u32[]{:S(2)}) collective-permute-start(bf16[12,64,128]{2,1,0:T(8,128)(2,1)S(1)} %get-tuple-element.34.refs_4_), channel_id=1, source_target_pairs={{0,192},{64,0},{128,64},{192,128},{1,193},{65,1},{129,65},{193,129... | collective-permute-start | bytes 589832 | tf_op jit(solution)/shard_map/ppermute | solution.py:236
  5.1 1.8 %collective-permute-start.1 = (bf16[12,64,128]{2,1,0:T(8,128)(2,1)S(1)}, bf16[12,64,128]{2,1,0:T(8,128)(2,1)}, u32[]{:S(2)}, u32[]{:S(2)}) collective-permute-start(bf16[12,64,128]{2,1,0:T(8,128)(2,1)S(1)} %get-tuple-element.35.refs_0_), channel_id=1, source_target_pairs={{0,192},{64,0},{128,64},{192,128},{1,193},{65,1},{129,65},{193,129... | collective-permute-start | bytes 589832 | tf_op jit(solution)/shard_map/ppermute | solution.py:238
  7.1 2.7 %collective-permute-done.refs_1_ = bf16[12,64,128]{2,1,0:T(8,128)(2,1)S(1)} collective-permute-done((bf16[12,64,128]{2,1,0:T(8,128)(2,1)S(1)}, bf16[12,64,128]{2,1,0:T(8,128)(2,1)S(1)}, u32[]{:S(2)}, u32[]{:S(2)}) %collective-permute-start) | collective-permute-done | bytes 196640 | tf_op jit(solution)/shard_map/ppermute | solution.py:235
  9.9 1.4 %collective-permute-start.2 = (bf16[12,64,128]{2,1,0:T(8,128)(2,1)S(1)}, bf16[12,64,128]{2,1,0:T(8,128)(2,1)}, u32[]{:S(2)}, u32[]{:S(2)}) collective-permute-start(bf16[12,64,128]{2,1,0:T(8,128)(2,1)S(1)} %collective-permute-done.refs_1_), channel_id=1, source_target_pairs={{0,64},{64,128},{128,192},{192,0},{1,65},{65,129},{129,193},{193,1... | collective-permute-start | bytes 589832 | tf_op jit(solution)/shard_map/ppermute | solution.py:239
  11.3 2.9 %collective-permute-start.5 = (bf16[12,64,128]{2,1,0:T(8,128)(2,1)}, bf16[12,64,128]{2,1,0:T(8,128)(2,1)}, u32[]{:S(2)}, u32[]{:S(2)}) collective-permute-start(bf16[12,64,128]{2,1,0:T(8,128)(2,1)} %collective-permute-done.4.refs_6_), channel_id=1, source_target_pairs={{0,192},{64,0},{128,64},{192,128},{1,193},{65,1},{129,65},{193,129... | collective-permute-start | bytes 589832 | tf_op jit(solution)/shard_map/ppermute | solution.py:240
  17.3 1.8 %shard_map.77 = (bf16[2,128,128]{2,1,0:T(8,128)(2,1)S(1)}, bf16[2,2,128,256]{3,2,1,0:T(8,128)(2,1)S(1)}) custom-call(bf16[128,4096]{1,0:T(8,128)(2,1)S(1)} %bitcast.14, bf16[128,4096]{1,0:T(8,128)(2,1)S(1)} %bitcast.17, f32[2,4096]{1,0:T(2,128)S(1)} %bitcast.20), custom_call_target="tpu_custom_call" | custom-call | flops 1000000000 | bytes 2129920 | tf_op jit(solution)/shard_map/pallas_call | solution.py:41
  19.2 2.6 %collective-permute-start.14 = (bf16[12,64,128]{2,1,0:T(8,128)(2,1)S(1)}, bf16[12,64,128]{2,1,0:T(8,128)(2,1)S(1)}, u32[]{:S(2)}, u32[]{:S(2)}) collective-permute-start(bf16[12,64,128]{2,1,0:T(8,128)(2,1)S(1)} %get-tuple-element.32.refs_4_), channel_id=1, source_target_pairs={{0,192},{64,0},{128,64},{192,128},{1,193},{65,1},{129,65},{193,129... | collective-permute-start | bytes 589832 | tf_op jit(solution)/shard_map/ppermute | solution.py:236
  21.8 2.3 %shard_map.78 = (bf16[33,2,64,128]{3,2,1,0:T(8,128)(2,1)S(1)}, bf16[33,2,64,128]{3,2,1,0:T(8,128)(2,1)S(1)}) custom-call(s32[1,24]{1,0:T(1,128)S(1)} %copy-done.4, s32[8,4]{1,0:T(8,128)S(1)} %copy.8.cos_ref, bf16[2,128,128]{2,1,0:T(8,128)(2,1)S(1)} %get-tuple-element.17.metric_ref, bf16[12,64,128]{2,1,0:T(8,128)(2,1)S(1)} %get-tuple-element.35.refs_0_, ...), custom_call_target="tpu_custom_call" | custom-call | flops 1000000000 | bytes 1638624 | tf_op jit(solution)/shard_map/pallas_call | solution.py:41
  24.3 2.0 %collective-permute-start.13 = (bf16[12,64,128]{2,1,0:T(8,128)(2,1)S(1)}, bf16[12,64,128]{2,1,0:T(8,128)(2,1)S(1)}, u32[]{:S(2)}, u32[]{:S(2)}) collective-permute-start(bf16[12,64,128]{2,1,0:T(8,128)(2,1)S(1)} %get-tuple-element.32.refs_4_), channel_id=1, source_target_pairs={{0,64},{64,128},{128,192},{192,0},{1,65},{65,129},{129,193},{193,1... | collective-permute-start | bytes 589832 | tf_op jit(solution)/shard_map/ppermute | solution.py:237
  27.0 3.2 %collective-permute-start.15 = (bf16[12,64,128]{2,1,0:T(8,128)(2,1)S(1)}, bf16[12,64,128]{2,1,0:T(8,128)(2,1)S(1)}, u32[]{:S(2)}, u32[]{:S(2)}) collective-permute-start(bf16[12,64,128]{2,1,0:T(8,128)(2,1)S(1)} %collective-permute-done.14.refs_6_), channel_id=1, source_target_pairs={{0,192},{64,0},{128,64},{192,128},{1,193},{65,1},{129,65},{193,129... | collective-permute-start | bytes 589832 | tf_op jit(solution)/shard_map/ppermute | solution.py:240
  30.2 1.8 %collective-permute-done.11.refs_2_ = bf16[12,64,128]{2,1,0:T(8,128)(2,1)S(1)} collective-permute-done((bf16[12,64,128]{2,1,0:T(8,128)(2,1)S(1)}, bf16[12,64,128]{2,1,0:T(8,128)(2,1)S(1)}, u32[]{:S(2)}, u32[]{:S(2)}) %collective-permute-start.11) | collective-permute-done | bytes 196640 | tf_op jit(solution)/shard_map/ppermute | solution.py:238
  32.1 1.3 %collective-permute-done.13.refs_5_ = bf16[12,64,128]{2,1,0:T(8,128)(2,1)S(1)} collective-permute-done((bf16[12,64,128]{2,1,0:T(8,128)(2,1)S(1)}, bf16[12,64,128]{2,1,0:T(8,128)(2,1)S(1)}, u32[]{:S(2)}, u32[]{:S(2)}) %collective-permute-start.13) | collective-permute-done | bytes 196640 | tf_op jit(solution)/shard_map/ppermute | solution.py:237
  33.4 3.6 %collective-permute-done.12.refs_3_ = bf16[12,64,128]{2,1,0:T(8,128)(2,1)S(1)} collective-permute-done((bf16[12,64,128]{2,1,0:T(8,128)(2,1)S(1)}, bf16[12,64,128]{2,1,0:T(8,128)(2,1)S(1)}, u32[]{:S(2)}, u32[]{:S(2)}) %collective-permute-start.12) | collective-permute-done | bytes 196640 | tf_op jit(solution)/shard_map/ppermute | solution.py:239
  38.8 2.6 %shard_map.82 = (bf16[33,2,64,128]{3,2,1,0:T(8,128)(2,1)}, bf16[33,2,64,128]{3,2,1,0:T(8,128)(2,1)S(1)}) custom-call(s32[1,24]{1,0:T(1,128)S(1)} %copy-done.4, s32[8,4]{1,0:T(8,128)S(1)} %copy.8.cos_ref, bf16[2,128,128]{2,1,0:T(8,128)(2,1)S(1)} %get-tuple-element.17.metric_ref, bf16[12,64,128]{2,1,0:T(8,128)(2,1)S(1)} %copy-done.1, ...), custom_call_target="tpu_custom_call" | custom-call | flops 1000000000 | bytes 1638624 | tf_op jit(solution)/shard_map/pallas_call | solution.py:41
  41.7 1.6 %collective-permute-start.7 = (bf16[8,2,64,128]{3,2,1,0:T(8,128)(2,1)S(1)}, bf16[8,2,64,128]{3,2,1,0:T(8,128)(2,1)S(1)}, u32[]{:S(2)}, u32[]{:S(2)}) collective-permute-start(bf16[8,2,64,128]{3,2,1,0:T(8,128)(2,1)S(1)} %get-tuple-element.21), channel_id=1, source_target_pairs={{0,16},{1,17},{2,18},{3,19},{4,20},{5,21},{6,22},{7,23},{8,24},{9,... | collective-permute-start | bytes 786440 | tf_op jit(solution)/shard_map/ppermute | solution.py:256
  43.2 2.5 %collective-permute-start.8 = (bf16[8,2,64,128]{3,2,1,0:T(8,128)(2,1)S(1)}, bf16[8,2,64,128]{3,2,1,0:T(8,128)(2,1)S(1)}, u32[]{:S(2)}, u32[]{:S(2)}) collective-permute-start(bf16[8,2,64,128]{3,2,1,0:T(8,128)(2,1)S(1)} %get-tuple-element.22), channel_id=1, source_target_pairs={{0,32},{1,33},{2,34},{3,35},{4,36},{5,37},{6,38},{7,39},{8,40},{9,... | collective-permute-start | bytes 786440 | tf_op jit(solution)/shard_map/ppermute | solution.py:256
  46.5 4.4 %collective-permute-done.7.b_ref = bf16[8,2,64,128]{3,2,1,0:T(8,128)(2,1)S(1)} collective-permute-done((bf16[8,2,64,128]{3,2,1,0:T(8,128)(2,1)S(1)}, bf16[8,2,64,128]{3,2,1,0:T(8,128)(2,1)S(1)}, u32[]{:S(2)}, u32[]{:S(2)}) %collective-permute-start.7) | collective-permute-done | bytes 262176 | tf_op jit(solution)/shard_map/ppermute | solution.py:256
  50.9 3.0 %collective-permute-done.8.c_ref = bf16[8,2,64,128]{3,2,1,0:T(8,128)(2,1)S(1)} collective-permute-done((bf16[8,2,64,128]{3,2,1,0:T(8,128)(2,1)S(1)}, bf16[8,2,64,128]{3,2,1,0:T(8,128)(2,1)S(1)}, u32[]{:S(2)}, u32[]{:S(2)}) %collective-permute-start.8) | collective-permute-done | bytes 262176 | tf_op jit(solution)/shard_map/ppermute | solution.py:256
  54.0 4.8 %collective-permute-done.9.d_ref = bf16[8,2,64,128]{3,2,1,0:T(8,128)(2,1)S(1)} collective-permute-done((bf16[8,2,64,128]{3,2,1,0:T(8,128)(2,1)S(1)}, bf16[8,2,64,128]{3,2,1,0:T(8,128)(2,1)S(1)}, u32[]{:S(2)}, u32[]{:S(2)}) %collective-permute-start.9) | collective-permute-done | bytes 262176 | tf_op jit(solution)/shard_map/ppermute | solution.py:256
  59.7 7.8 %all-to-all-start = ((bf16[8,2,64,128]{3,2,1,0:T(8,128)(2,1)}), bf16[8,2,64,128]{3,2,1,0:T(8,128)(2,1)S(1)}, u32[]{:S(2)}, u32[]{:S(2)}) async-start(bf16[8,2,64,128]{3,2,1,0:T(8,128)(2,1)} %shard_map.80), calls=%async_computation | async-start | bytes 524288 | tf_op jit(solution)/shard_map/all_to_all | solution.py:218
  67.5 1.5 %shard_map.83 = (bf16[8,2,64,128]{3,2,1,0:T(8,128)(2,1)S(1)}, bf16[8,2,64,128]{3,2,1,0:T(8,128)(2,1)S(1)}, bf16[8,2,64,128]{3,2,1,0:T(8,128)(2,1)S(1)}, bf16[8,2,64,128]{3,2,1,0:T(8,128)(2,1)S(1)}) custom-call(bf16[33,2,64,128]{3,2,1,0:T(8,128)(2,1)S(1)} %get-tuple-element.25.a_ref, bf16[33,2,64,128]{3,2,1,0:T(8,128)(2,1)} %collective-permute-done.16.b_ref), custom_call_target="tpu_custom_call" | custom-call | flops 10000000 | bytes 2162688 | tf_op jit(solution)/shard_map/pallas_call | solution.py:41
  69.0 1.4 %collective-permute-start.17 = (bf16[8,2,64,128]{3,2,1,0:T(8,128)(2,1)S(1)}, bf16[8,2,64,128]{3,2,1,0:T(8,128)(2,1)S(1)}, u32[]{:S(2)}, u32[]{:S(2)}) collective-permute-start(bf16[8,2,64,128]{3,2,1,0:T(8,128)(2,1)S(1)} %get-tuple-element.28), channel_id=1, source_target_pairs={{0,16},{1,17},{2,18},{3,19},{4,20},{5,21},{6,22},{7,23},{8,24},{9,... | collective-permute-start | bytes 786440 | tf_op jit(solution)/shard_map/ppermute | solution.py:256
  70.3 1.5 %collective-permute-start.18 = (bf16[8,2,64,128]{3,2,1,0:T(8,128)(2,1)S(1)}, bf16[8,2,64,128]{3,2,1,0:T(8,128)(2,1)S(1)}, u32[]{:S(2)}, u32[]{:S(2)}) collective-permute-start(bf16[8,2,64,128]{3,2,1,0:T(8,128)(2,1)S(1)} %get-tuple-element.29), channel_id=1, source_target_pairs={{0,32},{1,33},{2,34},{3,35},{4,36},{5,37},{6,38},{7,39},{8,40},{9,... | collective-permute-start | bytes 786440 | tf_op jit(solution)/shard_map/ppermute | solution.py:256
  71.8 1.7 %collective-permute-start.19 = (bf16[8,2,64,128]{3,2,1,0:T(8,128)(2,1)S(1)}, bf16[8,2,64,128]{3,2,1,0:T(8,128)(2,1)S(1)}, u32[]{:S(2)}, u32[]{:S(2)}) collective-permute-start(bf16[8,2,64,128]{3,2,1,0:T(8,128)(2,1)S(1)} %get-tuple-element.30), channel_id=1, source_target_pairs={{0,48},{1,49},{2,50},{3,51},{4,52},{5,53},{6,54},{7,55},{8,56},{9,... | collective-permute-start | bytes 786440 | tf_op jit(solution)/shard_map/ppermute | solution.py:256
  73.5 4.8 %collective-permute-done.17.b_ref = bf16[8,2,64,128]{3,2,1,0:T(8,128)(2,1)S(1)} collective-permute-done((bf16[8,2,64,128]{3,2,1,0:T(8,128)(2,1)S(1)}, bf16[8,2,64,128]{3,2,1,0:T(8,128)(2,1)S(1)}, u32[]{:S(2)}, u32[]{:S(2)}) %collective-permute-start.17) | collective-permute-done | bytes 262176 | tf_op jit(solution)/shard_map/ppermute | solution.py:256
  78.2 2.8 %collective-permute-done.18.c_ref = bf16[8,2,64,128]{3,2,1,0:T(8,128)(2,1)S(1)} collective-permute-done((bf16[8,2,64,128]{3,2,1,0:T(8,128)(2,1)S(1)}, bf16[8,2,64,128]{3,2,1,0:T(8,128)(2,1)S(1)}, u32[]{:S(2)}, u32[]{:S(2)}) %collective-permute-start.18) | collective-permute-done | bytes 262176 | tf_op jit(solution)/shard_map/ppermute | solution.py:256
  81.0 3.4 %collective-permute-done.19.d_ref = bf16[8,2,64,128]{3,2,1,0:T(8,128)(2,1)S(1)} collective-permute-done((bf16[8,2,64,128]{3,2,1,0:T(8,128)(2,1)S(1)}, bf16[8,2,64,128]{3,2,1,0:T(8,128)(2,1)S(1)}, u32[]{:S(2)}, u32[]{:S(2)}) %collective-permute-start.19) | collective-permute-done | bytes 262176 | tf_op jit(solution)/shard_map/ppermute | solution.py:256
  85.3 6.9 %all-to-all-start.1 = ((bf16[8,2,64,128]{3,2,1,0:T(8,128)(2,1)}), bf16[8,2,64,128]{3,2,1,0:T(8,128)(2,1)S(1)}, u32[]{:S(2)}, u32[]{:S(2)}) async-start(bf16[8,2,64,128]{3,2,1,0:T(8,128)(2,1)} %shard_map.84), calls=%async_computation.1 | async-start | bytes 524288 | tf_op jit(solution)/shard_map/all_to_all | solution.py:218
  92.3 12.0 %all-to-all-done.1.in_ref = bf16[8,2,64,128]{3,2,1,0:T(8,128)(2,1)S(1)} async-done(((bf16[8,2,64,128]{3,2,1,0:T(8,128)(2,1)}), bf16[8,2,64,128]{3,2,1,0:T(8,128)(2,1)S(1)}, u32[]{:S(2)}, u32[]{:S(2)}) %all-to-all-start.1) | async-done | bytes 262176 | tf_op jit(solution)/shard_map/all_to_all | solution.py:218
  105.1 1.8 %collective-permute-start.21 = (bf16[128,128]{1,0:T(8,128)(2,1)S(1)}, bf16[128,128]{1,0:T(8,128)(2,1)S(1)}, u32[]{:S(2)}, u32[]{:S(2)}) collective-permute-start(bf16[128,128]{1,0:T(8,128)(2,1)S(1)} %shard_map.86.a_ref), channel_id=1, source_target_pairs={{0,128},{64,192},{128,0},{192,64},{1,129},{65,193},{129,1},{193,65... | collective-permute-start | bytes 98312 | tf_op jit(solution)/shard_map/ppermute | solution.py:261
  108.1 2.9 %final.1 = bf16[2,128,2,2048]{3,2,1,0:T(2,128)(2,1)} custom-call(bf16[128,4096]{1,0:T(8,128)(2,1)S(1)} %bitcast.15, bf16[128,4096]{1,0:T(8,128)(2,1)S(1)} %bitcast.16, bf16[128,4096]{1,0:T(8,128)(2,1)S(1)} %bitcast.18, bf16[128,4096]{1,0:T(8,128)(2,1)S(1)} %bitcast.19, f32[2,4096]{1,0:T(2,128)S(1)} %bitcast.21, f32[2,4096]{1,0:T(2,128)S(1)} %bitcast.22, ...), custom_call_target="tpu_custom_call" | custom-call | flops 1000000000 | bytes 4194304 | tf_op jit(solution)/shard_map/final/pallas_call | solution.py:185
  (58 shorter events, 12.8 us)
Async XLA Ops:
  0.6 14.7 %copy-start.7 = (bf16[128,2,2048]{2,1,0:T(2,128)(2,1)S(1)}, bf16[128,2,2048]{2,1,0:T(2,128)(2,1)}, u32[]{:S(2)}) copy-start(bf16[128,2,2048]{2,1,0:T(2,128)(2,1)} %param.9) | copy-start | bytes 3145732
  1.8 8.1 %collective-permute-start = (bf16[12,64,128]{2,1,0:T(8,128)(2,1)S(1)}, bf16[12,64,128]{2,1,0:T(8,128)(2,1)S(1)}, u32[]{:S(2)}, u32[]{:S(2)}) collective-permute-start(bf16[12,64,128]{2,1,0:T(8,128)(2,1)S(1)} %get-tuple-element.35.refs_0_), channel_id=1, source_target_pairs={{0,64},{64,128},{128,192},{192,0},{1,65},{65,129},{129,193},{193,1... | collective-permute-start | bytes 589832 | tf_op jit(solution)/shard_map/ppermute | solution.py:235
  3.4 7.9 %collective-permute-start.4 = (bf16[12,64,128]{2,1,0:T(8,128)(2,1)S(1)}, bf16[12,64,128]{2,1,0:T(8,128)(2,1)}, u32[]{:S(2)}, u32[]{:S(2)}) collective-permute-start(bf16[12,64,128]{2,1,0:T(8,128)(2,1)S(1)} %get-tuple-element.34.refs_4_), channel_id=1, source_target_pairs={{0,192},{64,0},{128,64},{192,128},{1,193},{65,1},{129,65},{193,129... | collective-permute-start | bytes 589832 | tf_op jit(solution)/shard_map/ppermute | solution.py:236
  5.1 14.0 %collective-permute-start.1 = (bf16[12,64,128]{2,1,0:T(8,128)(2,1)S(1)}, bf16[12,64,128]{2,1,0:T(8,128)(2,1)}, u32[]{:S(2)}, u32[]{:S(2)}) collective-permute-start(bf16[12,64,128]{2,1,0:T(8,128)(2,1)S(1)} %get-tuple-element.35.refs_0_), channel_id=1, source_target_pairs={{0,192},{64,0},{128,64},{192,128},{1,193},{65,1},{129,65},{193,129... | collective-permute-start | bytes 589832 | tf_op jit(solution)/shard_map/ppermute | solution.py:238
  6.9 14.9 %collective-permute-start.3 = (bf16[12,64,128]{2,1,0:T(8,128)(2,1)S(1)}, bf16[12,64,128]{2,1,0:T(8,128)(2,1)}, u32[]{:S(2)}, u32[]{:S(2)}) collective-permute-start(bf16[12,64,128]{2,1,0:T(8,128)(2,1)S(1)} %get-tuple-element.34.refs_4_), channel_id=1, source_target_pairs={{0,64},{64,128},{128,192},{192,0},{1,65},{65,129},{129,193},{193,1... | collective-permute-start | bytes 589832 | tf_op jit(solution)/shard_map/ppermute | solution.py:237
  9.9 11.9 %collective-permute-start.2 = (bf16[12,64,128]{2,1,0:T(8,128)(2,1)S(1)}, bf16[12,64,128]{2,1,0:T(8,128)(2,1)}, u32[]{:S(2)}, u32[]{:S(2)}) collective-permute-start(bf16[12,64,128]{2,1,0:T(8,128)(2,1)S(1)} %collective-permute-done.refs_1_), channel_id=1, source_target_pairs={{0,64},{64,128},{128,192},{192,0},{1,65},{65,129},{129,193},{193,1... | collective-permute-start | bytes 589832 | tf_op jit(solution)/shard_map/ppermute | solution.py:239
  11.3 10.4 %collective-permute-start.5 = (bf16[12,64,128]{2,1,0:T(8,128)(2,1)}, bf16[12,64,128]{2,1,0:T(8,128)(2,1)}, u32[]{:S(2)}, u32[]{:S(2)}) collective-permute-start(bf16[12,64,128]{2,1,0:T(8,128)(2,1)} %collective-permute-done.4.refs_6_), channel_id=1, source_target_pairs={{0,192},{64,0},{128,64},{192,128},{1,193},{65,1},{129,65},{193,129... | collective-permute-start | bytes 589832 | tf_op jit(solution)/shard_map/ppermute | solution.py:240
  15.2 9.0 %copy-start = (bf16[12,64,128]{2,1,0:T(8,128)(2,1)}, bf16[12,64,128]{2,1,0:T(8,128)(2,1)S(1)}, u32[]{:S(2)}) copy-start(bf16[12,64,128]{2,1,0:T(8,128)(2,1)S(1)} %get-tuple-element.33.refs_0_) | copy-start | bytes 589828
  15.3 1.3 %copy-start.8 = (bf16[128,2,2048]{2,1,0:T(2,128)(2,1)S(1)}, bf16[128,2,2048]{2,1,0:T(2,128)(2,1)}, u32[]{:S(2)}) copy-start(bf16[128,2,2048]{2,1,0:T(2,128)(2,1)} %param.10) | copy-start | bytes 3145732
  15.3 11.1 %collective-permute-start.10 = (bf16[12,64,128]{2,1,0:T(8,128)(2,1)S(1)}, bf16[12,64,128]{2,1,0:T(8,128)(2,1)S(1)}, u32[]{:S(2)}, u32[]{:S(2)}) collective-permute-start(bf16[12,64,128]{2,1,0:T(8,128)(2,1)S(1)} %get-tuple-element.33.refs_0_), channel_id=1, source_target_pairs={{0,64},{64,128},{128,192},{192,0},{1,65},{65,129},{129,193},{193,1... | collective-permute-start | bytes 589832 | tf_op jit(solution)/shard_map/ppermute | solution.py:235
  15.7 1.2 %copy-start.9 = (f32[2,2,2048]{2,1,0:T(2,128)S(1)}, f32[2,2,2048]{2,1,0:T(2,128)}, u32[]{:S(2)}) copy-start(f32[2,2,2048]{2,1,0:T(2,128)} %param.11) | copy-start | bytes 98308
  17.3 4.5 %copy-start.4 = (s32[1,24]{1,0:T(1,128)S(1)}, s32[1,24]{1,0:T(1,128)}, u32[]{:S(2)}) copy-start(s32[1,24]{1,0:T(1,128)} %part_ref.3) | copy-start | bytes 292
  19.1 5.0 %copy-start.5 = (bf16[2,2,128,256]{3,2,1,0:T(8,128)(2,1)}, bf16[2,2,128,256]{3,2,1,0:T(8,128)(2,1)S(1)}, u32[]{:S(2)}) copy-start(bf16[2,2,128,256]{3,2,1,0:T(8,128)(2,1)S(1)} %get-tuple-element.31.gram_ref) | copy-start | bytes 786436
  19.2 7.9 %collective-permute-start.14 = (bf16[12,64,128]{2,1,0:T(8,128)(2,1)S(1)}, bf16[12,64,128]{2,1,0:T(8,128)(2,1)S(1)}, u32[]{:S(2)}, u32[]{:S(2)}) collective-permute-start(bf16[12,64,128]{2,1,0:T(8,128)(2,1)S(1)} %get-tuple-element.32.refs_4_), channel_id=1, source_target_pairs={{0,192},{64,0},{128,64},{192,128},{1,193},{65,1},{129,65},{193,129... | collective-permute-start | bytes 589832 | tf_op jit(solution)/shard_map/ppermute | solution.py:236
  24.1 17.3 %collective-permute-start.6 = (bf16[33,2,64,128]{3,2,1,0:T(8,128)(2,1)S(1)}, bf16[33,2,64,128]{3,2,1,0:T(8,128)(2,1)S(1)}, u32[]{:S(2)}, u32[]{:S(2)}) collective-permute-start(bf16[33,2,64,128]{3,2,1,0:T(8,128)(2,1)S(1)} %get-tuple-element.19), channel_id=1, source_target_pairs={{0,1},{1,0},{2,3},{3,2},{4,5},{5,4},{6,7},{7,6},{8,9},{9,8},{10,11... | collective-permute-start | bytes 3244040 | tf_op jit(solution)/shard_map/ppermute | solution.py:254
  24.2 7.8 %collective-permute-start.11 = (bf16[12,64,128]{2,1,0:T(8,128)(2,1)S(1)}, bf16[12,64,128]{2,1,0:T(8,128)(2,1)S(1)}, u32[]{:S(2)}, u32[]{:S(2)}) collective-permute-start(bf16[12,64,128]{2,1,0:T(8,128)(2,1)S(1)} %get-tuple-element.33.refs_0_), channel_id=1, source_target_pairs={{0,192},{64,0},{128,64},{192,128},{1,193},{65,1},{129,65},{193,129... | collective-permute-start | bytes 589832 | tf_op jit(solution)/shard_map/ppermute | solution.py:238
  24.3 9.0 %collective-permute-start.13 = (bf16[12,64,128]{2,1,0:T(8,128)(2,1)S(1)}, bf16[12,64,128]{2,1,0:T(8,128)(2,1)S(1)}, u32[]{:S(2)}, u32[]{:S(2)}) collective-permute-start(bf16[12,64,128]{2,1,0:T(8,128)(2,1)S(1)} %get-tuple-element.32.refs_4_), channel_id=1, source_target_pairs={{0,64},{64,128},{128,192},{192,0},{1,65},{65,129},{129,193},{193,1... | collective-permute-start | bytes 589832 | tf_op jit(solution)/shard_map/ppermute | solution.py:237
  26.3 10.6 %collective-permute-start.12 = (bf16[12,64,128]{2,1,0:T(8,128)(2,1)S(1)}, bf16[12,64,128]{2,1,0:T(8,128)(2,1)S(1)}, u32[]{:S(2)}, u32[]{:S(2)}) collective-permute-start(bf16[12,64,128]{2,1,0:T(8,128)(2,1)S(1)} %collective-permute-done.10.refs_1_), channel_id=1, source_target_pairs={{0,64},{64,128},{128,192},{192,0},{1,65},{65,129},{129,193},{193,1... | collective-permute-start | bytes 589832 | tf_op jit(solution)/shard_map/ppermute | solution.py:239
  27.0 9.9 %collective-permute-start.15 = (bf16[12,64,128]{2,1,0:T(8,128)(2,1)S(1)}, bf16[12,64,128]{2,1,0:T(8,128)(2,1)S(1)}, u32[]{:S(2)}, u32[]{:S(2)}) collective-permute-start(bf16[12,64,128]{2,1,0:T(8,128)(2,1)S(1)} %collective-permute-done.14.refs_6_), channel_id=1, source_target_pairs={{0,192},{64,0},{128,64},{192,128},{1,193},{65,1},{129,65},{193,129... | collective-permute-start | bytes 589832 | tf_op jit(solution)/shard_map/ppermute | solution.py:240
  41.4 26.1 %collective-permute-start.16 = (bf16[33,2,64,128]{3,2,1,0:T(8,128)(2,1)}, bf16[33,2,64,128]{3,2,1,0:T(8,128)(2,1)}, u32[]{:S(2)}, u32[]{:S(2)}) collective-permute-start(bf16[33,2,64,128]{3,2,1,0:T(8,128)(2,1)} %get-tuple-element.26), channel_id=1, source_target_pairs={{0,1},{1,0},{2,3},{3,2},{4,5},{5,4},{6,7},{7,6},{8,9},{9,8},{10,11... | collective-permute-start | bytes 3244040 | tf_op jit(solution)/shard_map/ppermute | solution.py:254
  41.7 9.3 %collective-permute-start.7 = (bf16[8,2,64,128]{3,2,1,0:T(8,128)(2,1)S(1)}, bf16[8,2,64,128]{3,2,1,0:T(8,128)(2,1)S(1)}, u32[]{:S(2)}, u32[]{:S(2)}) collective-permute-start(bf16[8,2,64,128]{3,2,1,0:T(8,128)(2,1)S(1)} %get-tuple-element.21), channel_id=1, source_target_pairs={{0,16},{1,17},{2,18},{3,19},{4,20},{5,21},{6,22},{7,23},{8,24},{9,... | collective-permute-start | bytes 786440 | tf_op jit(solution)/shard_map/ppermute | solution.py:256
  43.2 10.7 %collective-permute-start.8 = (bf16[8,2,64,128]{3,2,1,0:T(8,128)(2,1)S(1)}, bf16[8,2,64,128]{3,2,1,0:T(8,128)(2,1)S(1)}, u32[]{:S(2)}, u32[]{:S(2)}) collective-permute-start(bf16[8,2,64,128]{3,2,1,0:T(8,128)(2,1)S(1)} %get-tuple-element.22), channel_id=1, source_target_pairs={{0,32},{1,33},{2,34},{3,35},{4,36},{5,37},{6,38},{7,39},{8,40},{9,... | collective-permute-start | bytes 786440 | tf_op jit(solution)/shard_map/ppermute | solution.py:256
  45.7 13.1 %collective-permute-start.9 = (bf16[8,2,64,128]{3,2,1,0:T(8,128)(2,1)S(1)}, bf16[8,2,64,128]{3,2,1,0:T(8,128)(2,1)S(1)}, u32[]{:S(2)}, u32[]{:S(2)}) collective-permute-start(bf16[8,2,64,128]{3,2,1,0:T(8,128)(2,1)S(1)} %get-tuple-element.23), channel_id=1, source_target_pairs={{0,48},{1,49},{2,50},{3,51},{4,52},{5,53},{6,54},{7,55},{8,56},{9,... | collective-permute-start | bytes 786440 | tf_op jit(solution)/shard_map/ppermute | solution.py:256
  59.7 25.6 %all-to-all-start = ((bf16[8,2,64,128]{3,2,1,0:T(8,128)(2,1)}), bf16[8,2,64,128]{3,2,1,0:T(8,128)(2,1)S(1)}, u32[]{:S(2)}, u32[]{:S(2)}) async-start(bf16[8,2,64,128]{3,2,1,0:T(8,128)(2,1)} %shard_map.80), calls=%async_computation | async-start | bytes 524288 | tf_op jit(solution)/shard_map/all_to_all | solution.py:218
  69.0 9.3 %collective-permute-start.17 = (bf16[8,2,64,128]{3,2,1,0:T(8,128)(2,1)S(1)}, bf16[8,2,64,128]{3,2,1,0:T(8,128)(2,1)S(1)}, u32[]{:S(2)}, u32[]{:S(2)}) collective-permute-start(bf16[8,2,64,128]{3,2,1,0:T(8,128)(2,1)S(1)} %get-tuple-element.28), channel_id=1, source_target_pairs={{0,16},{1,17},{2,18},{3,19},{4,20},{5,21},{6,22},{7,23},{8,24},{9,... | collective-permute-start | bytes 786440 | tf_op jit(solution)/shard_map/ppermute | solution.py:256
  70.3 10.7 %collective-permute-start.18 = (bf16[8,2,64,128]{3,2,1,0:T(8,128)(2,1)S(1)}, bf16[8,2,64,128]{3,2,1,0:T(8,128)(2,1)S(1)}, u32[]{:S(2)}, u32[]{:S(2)}) collective-permute-start(bf16[8,2,64,128]{3,2,1,0:T(8,128)(2,1)S(1)} %get-tuple-element.29), channel_id=1, source_target_pairs={{0,32},{1,33},{2,34},{3,35},{4,36},{5,37},{6,38},{7,39},{8,40},{9,... | collective-permute-start | bytes 786440 | tf_op jit(solution)/shard_map/ppermute | solution.py:256
  71.8 12.6 %collective-permute-start.19 = (bf16[8,2,64,128]{3,2,1,0:T(8,128)(2,1)S(1)}, bf16[8,2,64,128]{3,2,1,0:T(8,128)(2,1)S(1)}, u32[]{:S(2)}, u32[]{:S(2)}) collective-permute-start(bf16[8,2,64,128]{3,2,1,0:T(8,128)(2,1)S(1)} %get-tuple-element.30), channel_id=1, source_target_pairs={{0,48},{1,49},{2,50},{3,51},{4,52},{5,53},{6,54},{7,55},{8,56},{9,... | collective-permute-start | bytes 786440 | tf_op jit(solution)/shard_map/ppermute | solution.py:256
  84.4 19.8 %copy-start.6 = (bf16[2,2,128,256]{3,2,1,0:T(8,128)(2,1)S(1)}, bf16[2,2,128,256]{3,2,1,0:T(8,128)(2,1)}, u32[]{:S(2)}) copy-start(bf16[2,2,128,256]{3,2,1,0:T(8,128)(2,1)} %copy-done.5) | copy-start | bytes 786436
  85.3 18.9 %all-to-all-start.1 = ((bf16[8,2,64,128]{3,2,1,0:T(8,128)(2,1)}), bf16[8,2,64,128]{3,2,1,0:T(8,128)(2,1)S(1)}, u32[]{:S(2)}, u32[]{:S(2)}) async-start(bf16[8,2,64,128]{3,2,1,0:T(8,128)(2,1)} %shard_map.84), calls=%async_computation.1 | async-start | bytes 524288 | tf_op jit(solution)/shard_map/all_to_all | solution.py:218
  104.5 6.5 %collective-permute-start.20 = (bf16[128,128]{1,0:T(8,128)(2,1)S(1)}, bf16[128,128]{1,0:T(8,128)(2,1)S(1)}, u32[]{:S(2)}, u32[]{:S(2)}) collective-permute-start(bf16[128,128]{1,0:T(8,128)(2,1)S(1)} %shard_map.86.a_ref), channel_id=1, source_target_pairs={{0,64},{64,128},{128,192},{192,0},{1,65},{65,129},{129,193},{193,1... | collective-permute-start | bytes 98312 | tf_op jit(solution)/shard_map/ppermute | solution.py:261
  105.1 5.9 %collective-permute-start.21 = (bf16[128,128]{1,0:T(8,128)(2,1)S(1)}, bf16[128,128]{1,0:T(8,128)(2,1)S(1)}, u32[]{:S(2)}, u32[]{:S(2)}) collective-permute-start(bf16[128,128]{1,0:T(8,128)(2,1)S(1)} %shard_map.86.a_ref), channel_id=1, source_target_pairs={{0,128},{64,192},{128,0},{192,64},{1,129},{65,193},{129,1},{193,65... | collective-permute-start | bytes 98312 | tf_op jit(solution)/shard_map/ppermute | solution.py:261
  107.0 4.1 %collective-permute-start.22 = (bf16[128,128]{1,0:T(8,128)(2,1)S(1)}, bf16[128,128]{1,0:T(8,128)(2,1)S(1)}, u32[]{:S(2)}, u32[]{:S(2)}) collective-permute-start(bf16[128,128]{1,0:T(8,128)(2,1)S(1)} %shard_map.86.a_ref), channel_id=1, source_target_pairs={{0,192},{64,0},{128,64},{192,128},{1,193},{65,1},{129,65},{193,129... | collective-permute-start | bytes 98312 | tf_op jit(solution)/shard_map/ppermute | solution.py:261
  (4 other events, 3.2 us)
